TPU v7x, 8 devices: a whole 2x2x1 slice. The times are simulated.
8 devices in a mesh: dp: 2 (over z, y), tp: 4 (over x, core).
Axes of the slice: x: 2, y: 2, z: 1, core: 2. Of those that a mesh axis runs over, the one named last changes fastest.
Arguments:
- x_norm: bfloat16 [4096, 3072], P(('dp', 'tp')), parts along dimension 0
- grad_y: bfloat16 [4096, 3072], P(('dp', 'tp')), parts along dimension 0
- u_gate: bfloat16 [4096, 8192], P('dp', 'tp'), parts along dimension 0
- u_up: bfloat16 [4096, 8192], P('dp', 'tp'), parts along dimension 0
- w_gate: bfloat16 [3072, 8192], P(None, 'tp')
- w_up: bfloat16 [3072, 8192], P(None, 'tp')
- w_down: bfloat16 [8192, 3072], P('tp')
- x_in: bfloat16 [4096, 3072], P(('dp', 'tp')), parts along dimension 0
- gamma: bfloat16 [3072], replicated
- grad_res: bfloat16 [4096, 3072], P(('dp', 'tp')), parts along dimension 0
- attn_out: bfloat16 [4096, 3072], P('dp', 'tp'), parts along dimension 0
- w_out: bfloat16 [3072, 3072], P('tp')
Outputs:
- output 1: bfloat16 [4096, 3072], P(('dp', 'tp')), parts along dimension 0
- output 2: bfloat16 [4096, 3072], P('dp', 'tp'), parts along dimension 0
- output 3: float32 [6144, 8192], P('dp', 'tp'), parts along dimension 0
- output 4: float32 [6144, 8192], P('dp', 'tp'), parts along dimension 0
- output 5: float32 [16384, 3072], P(('dp', 'tp')), parts along dimension 0
- output 6: float32 [6144, 3072], P(('dp', 'tp')), parts along dimension 0
There are 2 independent parts. A program takes and returns all parts, laid end to end along the dimension named above; an argument that names none is the same for every part.
All inputs are finite; a program needn't handle non-finite values.
Results may differ from a plain program's by a relative error of at most 0.0124445.
Values are sent between devices in bfloat16 or wider.
A program may use at most 1 GiB of HBM per device.

v0:
```python
import jax
import jax.numpy as jnp
from jax import lax
from jax.sharding import PartitionSpec as P

NORM_EPS = 1e-5
CONTRACT_ROWS = (((0,), (0,)), ((), ()))
CONTRACT_COLS = (((1,), (1,)), ((), ()))


def rms_backward(grad_x, x_in, gamma, grad_res):
    xin_f = x_in.astype(jnp.float32)
    inv_rms = lax.rsqrt(jnp.mean(xin_f * xin_f, axis=-1, keepdims=True) + NORM_EPS)
    scaled = grad_x.astype(jnp.float32) * gamma.astype(jnp.float32)
    proj_mean = jnp.mean(scaled * xin_f, axis=-1, keepdims=True)
    return (grad_res.astype(jnp.float32)
            + inv_rms * (scaled - xin_f * (inv_rms * inv_rms) * proj_mean)).astype(jnp.bfloat16)


def solution(mesh):
    token_spec = P(("dp", "tp"), None)
    split_cols = P("dp", "tp")
    weight_cols = P(None, "tp")
    weight_rows = P("tp", None)

    def local_backward(x_norm, grad_y, u_gate, u_up, w_gate, w_up, w_down, x_in, gamma, grad_res, attn_out, w_out):
        x_full = lax.all_gather(x_norm, "tp", axis=0, tiled=True)
        gy_full = lax.all_gather(grad_y, "tp", axis=0, tiled=True)
        gate_f = u_gate.astype(jnp.float32)
        up_f = u_up.astype(jnp.float32)
        sig_gate = jax.nn.sigmoid(gate_f)
        act_gate = gate_f * sig_gate
        silu_grad = sig_gate * (1.0 + gate_f * (1.0 - sig_gate))
        hidden_z = (act_gate * up_f).astype(jnp.bfloat16)
        gw_down = lax.dot_general(hidden_z, gy_full, CONTRACT_ROWS, preferred_element_type=jnp.float32)
        grad_h = lax.dot_general(gy_full, w_down, CONTRACT_COLS, preferred_element_type=jnp.float32)
        grad_up = (grad_h * act_gate).astype(jnp.bfloat16)
        grad_gate = (grad_h * up_f * silu_grad).astype(jnp.bfloat16)
        part_x = (lax.dot_general(grad_gate, w_gate, CONTRACT_COLS, preferred_element_type=jnp.float32)
                  + lax.dot_general(grad_up, w_up, CONTRACT_COLS, preferred_element_type=jnp.float32))
        grad_x = lax.psum_scatter(part_x.astype(jnp.bfloat16), "tp", scatter_dimension=0, tiled=True)
        gw_gate = lax.dot_general(x_full, grad_gate, CONTRACT_ROWS, preferred_element_type=jnp.float32)
        gw_up = lax.dot_general(x_full, grad_up, CONTRACT_ROWS, preferred_element_type=jnp.float32)
        grad_sum = rms_backward(grad_x, x_in, gamma, grad_res)
        gs_full = lax.all_gather(grad_sum, "tp", axis=0, tiled=True)
        grad_attn = lax.dot_general(gs_full, w_out, CONTRACT_COLS, preferred_element_type=jnp.float32).astype(jnp.bfloat16)
        gw_out = lax.dot_general(attn_out, gs_full, CONTRACT_ROWS, preferred_element_type=jnp.float32)
        return grad_sum, grad_attn, gw_gate, gw_up, gw_down, gw_out

    return jax.shard_map(
        local_backward,
        mesh=mesh,
        in_specs=(token_spec, token_spec, split_cols, split_cols, weight_cols, weight_cols, weight_rows,
                  token_spec, P(None), token_spec, split_cols, weight_rows),
        out_specs=(token_spec, split_cols, split_cols, split_cols, token_spec, token_spec),
        check_vma=False,
    )
```

profile of v0, /device:TPU:0, one launch (start us, length us, event | category | flops | bytes accessed | tf_op | source)
XLA Modules:
  0.0 461.3 jit_solution(1837887542175734743)
XLA Ops:
  7.2 0.0 copy-start
  7.2 0.0 all-gather.4.cloned.1.call-start
  7.2 0.7 all-gather.4.cloned.1.call-update
  7.9 0.0 all-gather.8.cloned.1.call-start
  8.0 0.7 all-gather.8.cloned.1.call-update
  8.7 0.0 reduce-scatter.2.cloned.1.call-start
  8.7 82.9 %all-gather.4.cloned.1.call-done = bf16[2048,3072]{1,0:T(8,128)(2,1)} async-done(((bf16[512,3072]{1,0:T(8,128)(2,1)}), bf16[2048,3072]{1,0:T(8,128)(2,1)}) %all-gather.4.cloned.1.call-update) | async-done | bytes 12582928 | tf_op jit(solution)/shard_map/all_gather | solution.py:28
  91.6 44.2 %fusion.1 = (bf16[2048,2048]{1,0:T(8,128)(2,1)}, f32[2048,2048]{1,0:T(8,128)}) fusion(bf16[2048,2048]{1,0:T(8,128)(2,1)} %param.15, bf16[2048,2048]{1,0:T(8,128)(2,1)} %param.14, bf16[2048,3072]{1,0:T(8,128)(2,1)} %all-gather.4.cloned.1.call-done, bf16[2048,3072]{1,0:T(8,128)(2,1)} %param.18), kind=kOutput, calls=%fused_computation.7 | convolution fusion | flops 25820135424 | bytes 67108864 | tf_op jit(solution)/shard_map/dot_general | solution.py:36
  135.8 34.8 %fusion.19 = f32[2048,3072]{1,0:T(8,128)} fusion(bf16[2048,2048]{1,0:T(8,128)(2,1)} %get-tuple-element.16, bf16[3072,2048]{1,0:T(8,128)(2,1)} %param.16), kind=kOutput, calls=%fused_computation.35 | convolution fusion | flops 25769803776 | bytes 46137344 | tf_op jit(solution)/shard_map/dot_general | solution.py:39
  170.6 37.1 %add_convert_fusion = bf16[2048,3072]{1,0:T(8,128)(2,1)} fusion(f32[2048,3072]{1,0:T(8,128)} %fusion.19, bf16[3072,2048]{1,0:T(8,128)(2,1)} %param.17, f32[2048,2048]{1,0:T(8,128)} %get-tuple-element.17, bf16[2048,2048]{1,0:T(8,128)(2,1)} %param.14), kind=kOutput, calls=%fused_computation | convolution fusion | flops 25811746816 | bytes 75497472 | tf_op jit(solution)/shard_map/dot_general | solution.py:40
  207.7 0.0 copy-start.1
  207.7 0.0 reduce-scatter.2.cloned.1.call-update
  207.7 0.0 all-gather.6.cloned.1.call-start
  207.8 0.6 copy-done.1
  208.4 0.0 all-gather.8.cloned.1.call-done
  208.4 36.3 %convolution_bitcast_fusion.1 = f32[3072,2048]{0,1:T(8,128)} fusion(bf16[2048,2048]{1,0:T(8,128)(2,1)} %get-tuple-element.16, bf16[2048,3072]{1,0:T(8,128)(2,1)} %all-gather.8.cloned.1.call-done), kind=kOutput, calls=%fused_computation.16 | convolution fusion | flops 25769803776 | bytes 46137344 | tf_op jit(solution)/shard_map/dot_general | solution.py:42
  244.7 24.9 %copy.18 = f32[3072,2048]{1,0:T(8,128)} copy(f32[3072,2048]{0,1:T(8,128)} %convolution_bitcast_fusion.1) | data formatting | bytes 50331648
  269.6 32.2 %reduce-scatter.2.cloned.1.call-done = bf16[512,3072]{1,0:T(8,128)(2,1)} async-done(((bf16[2048,3072]{1,0:T(8,128)(2,1)}), bf16[512,3072]{1,0:T(8,128)(2,1)}) %reduce-scatter.2.cloned.1.call-update) | async-done | bytes 3145744 | tf_op jit(solution)/shard_map/reduce_scatter | solution.py:41
  301.8 4.4 fusion.10
  306.2 6.3 %fusion.15 = bf16[512,3072]{1,0:T(8,128)(2,1)} fusion(bf16[512,3072]{1,0:T(8,128)(2,1)} %param.19, bf16[512,3072]{1,0:T(8,128)(2,1)} %reduce-scatter.2.cloned.1.call-done, bf16[512,3072]{1,0:T(8,128)(2,1)} %param.21, f32[512]{0:T(512)S(1)} %broadcast_multiply_fusion, f32[512]{0:T(512)S(1)} %get-tuple-element.15, f32[3072]{0:T(1024)S(1)} %convert_element_type.44, ...), kind=kLoop, calls=%fused_computation.26 | loop fusion | flops 15728640 | bytes 12601344 | tf_op jit(solution)/shard_map/convert_element_type | solution.py:17
  312.5 0.0 all-gather.6.cloned.1.call-update
  312.5 39.3 %convolution_bitcast_fusion = f32[3072,2048]{0,1:T(8,128)} fusion(bf16[2048,3072]{1,0:T(8,128)(2,1)} %all-gather.8.cloned.1.call-done, f32[2048,2048]{1,0:T(8,128)} %get-tuple-element.17, bf16[2048,2048]{1,0:T(8,128)(2,1)} %param.14), kind=kOutput, calls=%fused_computation.15 | convolution fusion | flops 25799163904 | bytes 62914560 | tf_op jit(solution)/shard_map/dot_general | solution.py:43
  351.8 24.7 %copy.19 = f32[3072,2048]{1,0:T(8,128)} copy(f32[3072,2048]{0,1:T(8,128)} %convolution_bitcast_fusion) | data formatting | bytes 50331648
  376.5 37.2 %fusion.8 = f32[2048,3072]{1,0:T(8,128)} fusion(bf16[2048,3072]{1,0:T(8,128)(2,1)} %all-gather.4.cloned.1.call-done, bf16[2048,2048]{1,0:T(8,128)(2,1)} %param.15, bf16[2048,2048]{1,0:T(8,128)(2,1)} %param.14), kind=kOutput, calls=%fused_computation.20 | convolution fusion | flops 25803358208 | bytes 54525952 | tf_op jit(solution)/shard_map/dot_general | solution.py:35
  413.7 0.0 all-gather.6.cloned.1.call-done
  413.7 0.0 copy-done
  413.7 15.2 %convolution_bitcast_fusion.2 = f32[768,3072]{0,1:T(8,128)} fusion(bf16[2048,3072]{1,0:T(8,128)(2,1)} %all-gather.6.cloned.1.call-done, bf16[2048,768]{1,0:T(8,128)(2,1)S(1)} %copy-done), kind=kOutput, calls=%fused_computation.29 | convolution fusion | flops 9663676416 | bytes 25165824 | tf_op jit(solution)/shard_map/dot_general | solution.py:47
  428.9 9.9 %copy.20 = f32[768,3072]{1,0:T(8,128)} copy(f32[768,3072]{0,1:T(8,128)} %convolution_bitcast_fusion.2) | data formatting | bytes 18874368
  438.8 15.4 %convolution_convert_fusion = bf16[2048,768]{1,0:T(8,128)(2,1)} fusion(bf16[2048,3072]{1,0:T(8,128)(2,1)} %all-gather.6.cloned.1.call-done, bf16[768,3072]{1,0:T(8,128)(2,1)} %param.23), kind=kOutput, calls=%fused_computation.30 | convolution fusion | flops 9665249280 | bytes 20447232 | tf_op jit(solution)/shard_map/dot_general | solution.py:46
  (3 shorter events, 0.0 us)
Async XLA Ops:
  7.2 406.5 %copy-start = (bf16[2048,768]{1,0:T(8,128)(2,1)S(1)}, bf16[2048,768]{1,0:T(8,128)(2,1)}, u32[]{:S(2)}) copy-start(bf16[2048,768]{1,0:T(8,128)(2,1)} %param.22) | copy-start | bytes 9437188
  7.2 84.5 %all-gather.4.cloned.1.call-start = ((), (), s32[]{:S(2)}) async-start(), calls=%async_computation.1 | async-start | bytes 15728640 | tf_op jit(solution)/shard_map/all_gather | solution.py:28
  7.9 200.5 %all-gather.8.cloned.1.call-start = ((), (), s32[]{:S(2)}) async-start(), calls=%async_computation.4 | async-start | bytes 15728640 | tf_op jit(solution)/shard_map/all_gather | solution.py:27
  8.7 293.2 %reduce-scatter.2.cloned.1.call-start = ((), (), s32[]{:S(2)}) async-start(), calls=%async_computation.2 | async-start | bytes 15728640 | tf_op jit(solution)/shard_map/reduce_scatter | solution.py:41
  207.7 0.7 copy-start.1
  207.7 206.0 %all-gather.6.cloned.1.call-start = ((), (), s32[]{:S(2)}) async-start(), calls=%async_computation.3 | async-start | bytes 15728640 | tf_op jit(solution)/shard_map/all_gather | solution.py:45
Sparse Core Ops, SparseCore 0:
  9.5 82.0 all-gather.3
  93.2 79.2 all-gather.7
  207.8 93.9 reduce-scatter.1
  312.6 79.2 all-gather.5
where the time goes:
time: 468 us; the launch traced here: 461 us
  matrix products  260 us (56%)
  waiting for transfers between devices  117 us (25%)
  local copies, waits for them, and re-layouts  60.1 us (13%)
  between operations  14.3 us (3%)
  other arithmetic  10.6 us (2%)
    all_gather x1, waiting for transfers between devices, local_backward(): gy_full = lax.all_gather(grad_y, 'tp', axis=0, tiled=True)  82.9 us
    unnamed x7, local copies, waits for them, and re-layouts  60.1 us
    dot_general x1, matrix products, local_backward(): lax.dot_general(gy_full, w_down, CONTRACT_COLS, preferred_element_type=jn...  44.2 us
    dot_general x1, matrix products, local_backward(): lax.dot_general(x_full, grad_up, CONTRACT_ROWS, preferred_element_type=jn...  39.3 us
    dot_general x1, matrix products, local_backward(): lax.dot_general(hidden_z, gy_full, CONTRACT_ROWS, preferred_element_type=...  37.2 us
    dot_general x1, matrix products, local_backward(): lax.dot_general(grad_up, w_up, CONTRACT_COLS, preferred_element_type=jnp....  37.1 us
    dot_general x1, matrix products, local_backward(): lax.dot_general(x_full, grad_gate, CONTRACT_ROWS, preferred_element_type=...  36.3 us
    dot_general x1, matrix products, local_backward(): lax.dot_general(grad_gate, w_gate, CONTRACT_COLS, preferred_element_type=...  34.8 us
  transfers between devices with their start and end apart: 4, of which 2 were waited for; matrix products, arithmetic and copies ran while one was open for 60% of the time, Pallas kernels for 0%

commit v1 on v0

v1 whole, which is shorter than its diff:
```python
import functools

import jax
import jax.numpy as jnp
from jax import lax
from jax.experimental import pallas as pl
from jax.experimental.pallas import tpu as pltpu
from jax.sharding import PartitionSpec as P


NORM_EPS = 1e-5
F32 = jnp.float32
BF16 = jnp.bfloat16
NT = (((1,), (1,)), ((), ()))
TN = (((0,), (0,)), ((), ()))
VMEM_LIMIT = 67043328


def call(kernel, grid, in_specs, out_specs, out_shape, flops, nbytes, scratch=(), after=(), offs=None, aliases=None, keep_offs=False):
    n_in, n_after = len(in_specs), len(after)
    n_pre = 0 if offs is None else 1

    def body(*refs):
        pre, refs = refs[:n_pre], refs[n_pre:]
        kernel(*(pre if keep_offs else ()), *refs[:n_in], *refs[n_in + n_after:])

    def run(*args):
        pre = () if offs is None else (offs,)
        return launch(pre, args)

    def launch(pre, args):
        return pl.pallas_call(
            body,
            grid_spec=pltpu.PrefetchScalarGridSpec(
                num_scalar_prefetch=n_pre,
                grid=grid,
                in_specs=list(in_specs) + [pl.BlockSpec(memory_space=pl.ANY)] * n_after,
                out_specs=out_specs,
                scratch_shapes=list(scratch),
            ),
            out_shape=out_shape,
            input_output_aliases={n_pre + i: o for i, o in (aliases or {}).items()},
            compiler_params=pltpu.CompilerParams(
                vmem_limit_bytes=VMEM_LIMIT, dimension_semantics=("arbitrary",) * len(grid)
            ),
            cost_estimate=pl.CostEstimate(flops=flops, bytes_accessed=nbytes, transcendentals=0),
        )(*pre, *args, *after)

    return run


def input_grads(pieces, starts, w_down, w_gate, w_up, u_gate, u_up, offs, cols, x_cols, after=()):
    rows, width = pieces[0].shape
    n_cols = w_down.shape[0]
    total = 2 * rows
    n_gate, n_x = n_cols // cols, width // x_cols

    def kernel(y0, y1, wd, g0, g1, u0, u1, wg, wu, o_gate, o_up, o_z, o_x0, o_x1, s_gate, s_up):
        step = pl.program_id(0)

        @pl.when(step < n_gate)
        def _():
            at = pl.ds(pl.multiple_of(step * cols, cols), cols)
            grad_y = jnp.concatenate([y0[...], y1[...]], axis=0)
            grad_h = lax.dot_general(grad_y, wd[...], NT, preferred_element_type=F32)
            gate_f = jnp.concatenate([g0[...], g1[...]], axis=0).astype(F32)
            up_f = jnp.concatenate([u0[...], u1[...]], axis=0).astype(F32)
            sig = jax.nn.sigmoid(gate_f)
            act = gate_f * sig
            d_up = (grad_h * act).astype(BF16)
            d_gate = (grad_h * up_f * (sig * (1.0 + gate_f * (1.0 - sig)))).astype(BF16)
            o_z[...] = (act * up_f).astype(BF16)
            o_up[...] = d_up
            o_gate[...] = d_gate
            s_up[:, at] = d_up
            s_gate[:, at] = d_gate

        @pl.when(step >= n_gate)
        def _():
            part = (lax.dot_general(s_gate[...], wg[...], NT, preferred_element_type=F32)
                    + lax.dot_general(s_up[...], wu[...], NT, preferred_element_type=F32)).astype(BF16)
            o_x0[...] = part[:rows]
            o_x1[...] = part[rows:]

    first = lambda j: jnp.minimum(j, n_gate - 1)
    second = lambda j: jnp.maximum(j - n_gate, 0)
    whole = pl.BlockSpec((rows, width), lambda j, o: (0, 0))
    tiles = [pl.BlockSpec((rows, cols), functools.partial(lambda s, j, o: (s(o), first(j)), s)) for s in starts]
    w_x = pl.BlockSpec((x_cols, n_cols), lambda j, o: (second(j), 0))
    out = pl.BlockSpec((total, cols), lambda j, o: (0, first(j)))
    out_x = pl.BlockSpec((rows, x_cols), lambda j, o: (0, second(j)))
    return call(
        kernel, (n_gate + n_x,),
        [whole, whole, pl.BlockSpec((cols, width), lambda j, o: (first(j), 0)), *tiles, *tiles, w_x, w_x],
        [out] * 3 + [out_x] * 2,
        [jax.ShapeDtypeStruct((total, n_cols), BF16)] * 3 + [jax.ShapeDtypeStruct((rows, width), BF16)] * 2,
        6 * total * width * n_cols, 2 * n_cols * (3 * width + 5 * total),
        scratch=[pltpu.VMEM((total, n_cols), BF16)] * 2, after=after, offs=offs,
    )(*pieces, w_down, u_gate, u_gate, u_up, u_up, w_gate, w_up)


def gw_in(x_parts, gates, ups, span, prev, rows, cols, after=()):
    width = x_parts[0].shape[1]
    n_tok = sum(x.shape[0] for x in x_parts)
    n_cols = gates[0].shape[1]
    half = gates[1].shape[0] // 2
    start, count = span[0] // rows, (span[1] - span[0]) // rows

    def kernel(*refs):
        x_own, x_par, x_acr, x_dia = (r[...] for r in refs[:4])
        x = [jnp.concatenate([x_own, x_par], axis=0)]
        x += [jnp.concatenate([x_acr[c * half:(c + 1) * half], x_dia[c * half:(c + 1) * half]], axis=0) for c in range(2)]
        for ds, out in ((refs[4:7], refs[-2]), (refs[7:10], refs[-1])):
            total = None
            for a, d in zip(x, ds):
                term = lax.dot_general(a, d[...], TN, preferred_element_type=F32)
                total = term if total is None else total + term
            out[...] = total

    in_specs = [pl.BlockSpec((x.shape[0], rows), lambda i, j: (0, start + i)) for x in x_parts]
    in_specs += [pl.BlockSpec((d.shape[0], cols), lambda i, j: (0, j)) for d in (*gates, *ups)]
    args = [*x_parts, *gates, *ups]
    aliases = None
    if prev is not None:
        in_specs += [pl.BlockSpec(memory_space=pl.ANY)] * 2
        args += list(prev)
        aliases = {10: 0, 11: 1}
    return call(
        kernel, (count, n_cols // cols), in_specs,
        [pl.BlockSpec((rows, cols), lambda i, j: (start + i, j))] * 2,
        [jax.ShapeDtypeStruct((width, n_cols), F32)] * 2,
        4 * n_tok * (span[1] - span[0]) * n_cols, 8 * (span[1] - span[0]) * n_cols, after=after, aliases=aliases,
    )(*args)


def gw_down(zs, y_pairs, rows, cols, after=()):
    n_rows = zs[0].shape[1]
    width = y_pairs[0][0].shape[1]
    flat = [y for pair in y_pairs for y in pair]
    n_tok = sum(z.shape[0] for z in zs)

    def kernel(z0, z1, z2, a0, b0, a1, b1, a2, b2, out):
        total = None
        for z, a, b in ((z0, a0, b0), (z1, a1, b1), (z2, a2, b2)):
            y = jnp.concatenate([a[...], b[...]], axis=0)
            term = lax.dot_general(z[...], y, TN, preferred_element_type=F32)
            total = term if total is None else total + term
        out[...] = total

    return call(
        kernel, (n_rows // rows, width // cols),
        [pl.BlockSpec((z.shape[0], rows), lambda i, j: (0, i)) for z in zs]
        + [pl.BlockSpec((y.shape[0], cols), lambda i, j: (0, j)) for y in flat],
        pl.BlockSpec((rows, cols), lambda i, j: (i, j)),
        jax.ShapeDtypeStruct((n_rows, width), F32),
        2 * n_tok * width * n_rows, 4 * width * n_rows, after=after,
    )(*zs, *flat)


def head_rows(x, start, rows, block=128, after=()):
    width = x.shape[1]
    first = start // block

    def kernel(src, out):
        out[...] = src[...]

    return call(
        kernel, (rows // block,), [pl.BlockSpec((block, width), lambda i: (first + i, 0))],
        pl.BlockSpec((block, width), lambda i: (i, 0)), jax.ShapeDtypeStruct((rows, width), x.dtype),
        rows * width, rows * width * 4, after=after,
    )(x)


def norm_chunk(parts, starts, rows, first_row, x_in, gamma, grad_res, prev, cuts, block=128, after=()):
    width = x_in.shape[1]
    n_cuts = len(cuts)
    edges = [sum(cuts[:k]) // block for k in range(n_cuts + 1)]

    def kernel(p0, p1, p2, xin, gam, res, *outs):
        outs = outs[-1 - n_cuts:]
        grad_x = (p0[...].astype(F32) + p1[...].astype(F32) + p2[...].astype(F32)).astype(BF16).astype(F32)
        xin_f = xin[...].astype(F32)
        inv_rms = lax.rsqrt(jnp.mean(xin_f * xin_f, axis=-1, keepdims=True) + NORM_EPS)
        scaled = grad_x * gam[...].astype(F32)
        proj_mean = jnp.mean(scaled * xin_f, axis=-1, keepdims=True)
        out = (res[...].astype(F32) + inv_rms * (scaled - xin_f * (inv_rms * inv_rms) * proj_mean)).astype(BF16)
        outs[-1][...] = out
        for k in range(n_cuts):
            @pl.when((pl.program_id(0) >= edges[k]) & (pl.program_id(0) < edges[k + 1]))
            def _(k=k):
                outs[k][...] = out

    first = first_row // block
    at = lambda s: pl.BlockSpec((block, width), lambda i: (s + i, 0))
    cut = lambda k: pl.BlockSpec((block, width), lambda i: (jnp.clip(i - edges[k], 0, edges[k + 1] - edges[k] - 1), 0))
    in_specs = [at(s // block) for s in starts] + [at(first), pl.BlockSpec((1, width), lambda i: (0, 0)), at(first)]
    args = [*parts, x_in, gamma, grad_res]
    aliases = None
    if prev is not None:
        in_specs.append(pl.BlockSpec(memory_space=pl.ANY))
        args.append(prev)
        aliases = {len(in_specs) - 1: n_cuts}
    return call(
        kernel, (rows // block,), in_specs, [cut(k) for k in range(n_cuts)] + [at(first)],
        [jax.ShapeDtypeStruct((c, width), BF16) for c in cuts] + [jax.ShapeDtypeStruct(x_in.shape, BF16)],
        rows * width * 20, rows * width * 14, after=after, aliases=aliases,
    )(*args)


def grad_attention(pieces, at_rows, blocks, w_out, offs, n_tok, after=()):
    n_cols, width = w_out.shape
    n = len(pieces)
    size = n_tok // 8

    def kernel(*refs):
        srcs, w, out = refs[:n], refs[n], refs[-1]
        for q in range(n):
            @pl.when(pl.program_id(0) == q)
            def _(q=q):
                out[...] = lax.dot_general(srcs[q][...], w[...], NT, preferred_element_type=F32).astype(BF16)

    def out_map(j, o):
        row = blocks[0](o)
        for q in range(1, n):
            row = jnp.where(j >= q, blocks[q](o), row)
        return (row, 0)

    return call(
        kernel, (n,),
        [pl.BlockSpec((size, width), functools.partial(lambda r, j, o: (r, 0), r)) for r in at_rows]
        + [pl.BlockSpec((n_cols, width), lambda j, o: (0, 0))],
        pl.BlockSpec((size, n_cols), out_map), jax.ShapeDtypeStruct((n_tok, n_cols), BF16),
        2 * n * size * width * n_cols, 2 * width * n_cols, after=after, offs=offs,
    )(*pieces, w_out)


def out_grads(pieces, blocks, todo, attn_out, w_out, offs, d_attn, cols, after=()):
    n_tok, n_rows = attn_out.shape
    width = w_out.shape[1]
    n = len(pieces)
    sizes = [p.shape[0] for p in pieces]
    left = sum(sizes[q] for q in todo)
    last = width // cols - 1

    def kernel(offs_ref, *refs):
        srcs, attn, w = refs[:n], refs[n:2 * n], refs[2 * n]
        o_attn, o_w, acc, done, sem = refs[-5:]
        step = pl.program_id(0)
        term = lax.dot_general(jnp.concatenate([srcs[q][...] for q in todo], axis=0), w[...], NT, preferred_element_type=F32)
        lhs = jnp.concatenate([a[...] for a in attn], axis=0)
        rhs = jnp.concatenate([src[...] for src in srcs], axis=0)
        o_w[...] = lax.dot_general(lhs, rhs, TN, preferred_element_type=F32)

        @pl.when(step == 0)
        def _():
            acc[...] = term

        @pl.when((step > 0) & (step < last))
        def _():
            acc[...] += term

        @pl.when(step == last)
        def _():
            done[...] = (acc[...] + term).astype(BF16)
            copies, first = [], 0
            for k, q in enumerate(todo):
                row = pl.multiple_of(blocks[q](offs_ref) * sizes[q], sizes[q])
                copies.append(pltpu.make_async_copy(
                    done.at[pl.ds(first, sizes[q])], o_attn.at[pl.ds(row, sizes[q])], sem.at[k]))
                copies[-1].start()
                first += sizes[q]
            for copy in copies:
                copy.wait()

    in_specs = [pl.BlockSpec((r, cols), lambda j, o: (0, j)) for r in sizes]
    in_specs += [pl.BlockSpec((r, n_rows), functools.partial(lambda m, j, o: (m(o), 0), m)) for r, m in zip(sizes, blocks)]
    in_specs += [pl.BlockSpec((n_rows, cols), lambda j, o: (0, j)), pl.BlockSpec(memory_space=pl.ANY)]
    return call(
        kernel, (width // cols,), in_specs,
        [pl.BlockSpec(memory_space=pl.ANY), pl.BlockSpec((n_rows, cols), lambda j, o: (0, j))],
        [jax.ShapeDtypeStruct((n_tok, n_rows), BF16), jax.ShapeDtypeStruct((n_rows, width), F32)],
        2 * (n_tok + left) * width * n_rows, 4 * width * n_rows, after=after, offs=offs, keep_offs=True,
        aliases={2 * n + 1: 0},
        scratch=[pltpu.VMEM((left, n_rows), F32), pltpu.VMEM((left, n_rows), BF16), pltpu.SemaphoreType.DMA((len(todo),))],
    )(*pieces, *([attn_out] * n), w_out, d_attn)


def solution(mesh):
    token_spec = P(("dp", "tp"), None)
    split_cols = P("dp", "tp")
    weight_cols = P(None, "tp")
    weight_rows = P("tp", None)
    partner = [(i, i ^ 1) for i in range(4)]
    across = [(i, i ^ 2) for i in range(4)]

    def swap(x):
        return lax.ppermute(x, "tp", partner)

    def send(x):
        return lax.ppermute(x, "tp", across)

    def backward(x_norm, grad_y, u_gate, u_up, w_gate, w_up, w_down, x_in, gamma, grad_res, attn_out, w_out):
        own, width = grad_y.shape
        half = own // 2
        n_tok = u_gate.shape[0]
        offs = lax.axis_index("tp") ^ jnp.arange(4, dtype=jnp.int32)
        gain = gamma.reshape(1, width)
        of = lambda p, c: (lambda o: 2 * o[p] + c)
        weights = (w_down, w_gate, w_up, u_gate, u_up, offs)

        y_par = swap(grad_y)
        head0 = head_rows(grad_y, 0, half)
        head1 = head_rows(grad_y, half, half, after=(head0,))
        y_acr = [send(head0), send(head1)]
        y_dia = [swap(y_acr[c]) for c in range(2)]
        x_par = swap(x_norm)
        x_acr = send(x_norm)
        x_dia = swap(x_acr)
        x_parts = (x_norm, x_par, x_acr, x_dia)

        g_l, u_l, z_l, dx_own, dx_par = input_grads(
            (grad_y, y_par), (lambda o: o[0], lambda o: o[1]), *weights, 256, 512, after=(gain, head1))
        dx_sib = swap(dx_par)
        gates, ups, zs, dx_rem = [g_l], [u_l], [z_l], []
        last = dx_own
        for c in range(2):
            g, u, z, to_acr, to_dia = input_grads(
                (y_acr[c], y_dia[c]), (of(2, c), of(3, c)), *weights, 512, 512, after=(last,))
            dx_rem.append((to_acr, swap(to_dia)))
            last = to_acr
            gates.append(g)
            ups.append(u)
            zs.append(z)
        both = [(a.astype(F32) + b.astype(F32)).astype(BF16) for a, b in dx_rem]
        rs = [send(both[c]) for c in range(2)]

        gwd = gw_down(zs, ((grad_y, y_par), (y_acr[0], y_dia[0]), (y_acr[1], y_dia[1])), 1024, 512, after=(both[0],))
        third = width // 3
        norm = (x_in, gain, grad_res)
        gw = gw_in(x_parts, gates, ups, (0, third), None, 1024, 512, after=(gwd, both[1]))
        ds0, ds = norm_chunk((dx_own, dx_sib, rs[0]), (0, 0, 0), half, 0, *norm, None, (half,), after=(gw[0],))
        s_acr0, s_par0 = send(ds0), swap(ds0)
        gw = gw_in(x_parts, gates, ups, (third, 2 * third), gw, 1024, 512, after=(ds0,))
        ds1, ds = norm_chunk((dx_own, dx_sib, rs[1]), (half, half, 0), half, half, *norm, ds, (half,), after=(gw[0],))
        s_acr1, s_par1 = send(ds1), swap(ds1)
        gwg, gwu = gw_in(x_parts, gates, ups, (2 * third, width), gw, 1024, 512, after=(ds1,))
        s_dia0, s_dia1 = swap(s_acr0), swap(s_acr1)

        d_attn = grad_attention((ds, ds, s_par0, s_par1, s_acr0, s_dia0), (0, 1, 0, 0, 0, 0),
                                (of(0, 0), of(0, 1), of(1, 0), of(1, 1), of(2, 0), of(3, 0)), w_out, offs, n_tok, after=(gwg,))
        d_attn, gwo = out_grads((ds, s_par0, s_par1, s_acr0, s_dia0, s_acr1, s_dia1),
                                (lambda o: o[0], of(1, 0), of(1, 1), of(2, 0), of(3, 0), of(2, 1), of(3, 1)), (5, 6),
                                attn_out, w_out, offs, d_attn, 512)
        return ds, d_attn, gwg, gwu, gwd, gwo

    return jax.shard_map(
        backward,
        mesh=mesh,
        in_specs=(token_spec, token_spec, split_cols, split_cols, weight_cols, weight_cols, weight_rows,
                  token_spec, P(None), token_spec, split_cols, weight_rows),
        out_specs=(token_spec, split_cols, split_cols, split_cols, token_spec, token_spec),
        check_vma=False,
    )
```

time: 468 us -> 427 us (0.912); the launches traced: 461 us -> 427 us
  Pallas kernels: 0 us -> 274 us
  matrix products: 260 us -> 0 us
  local copies, waits for them, and re-layouts: 60.1 us -> 1.3 us
  waiting for transfers between devices: 117 us -> 133 us
  between operations: 14.3 us -> 0.91 us
  starting transfers between devices: 0.16 us -> 11.5 us
    pallas_call x0 -> x13, Pallas kernels: none -> 274 us  [launch(): pl.pallas_call(body, grid_spec=pltpu.PrefetchScalarGridSpec(num_scalar_pr...]
    dot_general x8 -> x0, matrix products: 260 us -> none  [the longest x1 44.2 us: local_backward(): lax.dot_general(gy_full, w_down, CONTRACT_COLS, preferred_element_type=jn...]
    ppermute x0 -> x19, waiting for transfers between devices: none -> 133 us  [the longest x7 133 us: send(): return lax.ppermute(x, 'tp', across)]
    all_gather x3 -> x0, waiting for transfers between devices: 82.9 us -> none  [the longest x1 82.9 us: local_backward(): gy_full = lax.all_gather(grad_y, 'tp', axis=0, tiled=True)]
    unnamed x7 -> x2, local copies, waits for them, and re-layouts: 60.1 us -> 0.01 us
    reduce_scatter x1 -> x0, waiting for transfers between devices: 32.2 us -> none  [local_backward(): lax.psum_scatter(part_x.astype(jnp.bfloat16), 'tp', scatter_dimension=0,...]
    ppermute x0 -> x19, starting transfers between devices: none -> 11.5 us  [the longest x7 8.6 us: send(): return lax.ppermute(x, 'tp', across)]
  transfers between devices with their start and end apart: 4 -> 19, of which waited for: 2 -> 4; matrix products, arithmetic and copies ran while one was open for 60% -> 2% of each run, Pallas kernels for 0% -> 58%
where the time goes in v1:
time: 427 us
  Pallas kernels  274 us (64%)
  waiting for transfers between devices  133 us (31%)
  starting transfers between devices  11.5 us (3%)
  other arithmetic  5.94 us (1%)
    pallas_call x13, Pallas kernels, launch(): pl.pallas_call(body, grid_spec=pltpu.PrefetchScalarGridSpec(num_scalar_pr...  274 us
    ppermute x7, waiting for transfers between devices, send(): return lax.ppermute(x, 'tp', across)  133 us
    ppermute x7, starting transfers between devices, send(): return lax.ppermute(x, 'tp', across)  8.6 us
  transfers between devices with their start and end apart: 19, of which 4 were waited for; matrix products, arithmetic and copies ran while one was open for 2% of the time, Pallas kernels for 58%

profile of v1, /device:TPU:0, one launch (start us, length us, event | category | flops | bytes accessed | tf_op | source)
XLA Modules:
  0.0 427.0 jit_solution(5460798590154960972)
XLA Ops:
  0.6 0.9 collective-permute-start
  1.5 2.3 shard_map.163.refs_1_
  3.8 2.3 shard_map.164.refs_11_
  6.1 2.5 collective-permute-start.2
  8.7 2.0 collective-permute-start.11
  10.7 1.3 reshape.15.refs_10_.refs_4_
  12.0 0.6 iota_xor_fusion.refs_0_
  12.5 31.7 %collective-permute-done.2.refs_1_.refs_7_ = bf16[256,3072]{1,0:T(8,128)(2,1)} collective-permute-done((bf16[256,3072]{1,0:T(8,128)(2,1)}, bf16[256,3072]{1,0:T(8,128)(2,1)}, u32[]{:S(2)}, u32[]{:S(2)}) %collective-permute-start.2) | collective-permute-done | bytes 1572896 | tf_op jit(solution)/shard_map/ppermute | solution.py:300
  44.2 33.7 %collective-permute-done.4.refs_1_.refs_5_ = bf16[256,3072]{1,0:T(8,128)(2,1)} collective-permute-done((bf16[256,3072]{1,0:T(8,128)(2,1)}, bf16[256,3072]{1,0:T(8,128)(2,1)}, u32[]{:S(2)}, u32[]{:S(2)}) %collective-permute-start.4) | collective-permute-done | bytes 1572896 | tf_op jit(solution)/shard_map/ppermute | solution.py:300
  77.9 52.7 %shard_map.165 = (bf16[1024,2048]{1,0:T(8,128)(2,1)}, bf16[1024,2048]{1,0:T(8,128)(2,1)}, bf16[1024,2048]{1,0:T(8,128)(2,1)}, bf16[512,3072]{1,0:T(8,128)(2,1)}, bf16[512,3072]{1,0:T(8,128)(2,1)}) custom-call(s32[4]{0:T(128)} %iota_xor_fusion.refs_0_, bf16[512,3072]{1,0:T(8,128)(2,1)} %refs_3_.9, bf16[512,3072]{1,0:T(8,128)(2,1)} %collective-permute-done.refs_2_.refs_4_, ...), custom_call_target="tpu_custom_call" | custom-call | flops 38654705664 | bytes 58720256 | tf_op jit(solution)/shard_map/pallas_call | solution.py:32
  130.6 30.9 %shard_map.166 = (bf16[512,2048]{1,0:T(8,128)(2,1)}, bf16[512,2048]{1,0:T(8,128)(2,1)}, bf16[512,2048]{1,0:T(8,128)(2,1)}, bf16[256,3072]{1,0:T(8,128)(2,1)}, bf16[256,3072]{1,0:T(8,128)(2,1)}) custom-call(s32[4]{0:T(128)} %iota_xor_fusion.refs_0_, bf16[256,3072]{1,0:T(8,128)(2,1)} %collective-permute-done.4.refs_1_.refs_5_, ...), custom_call_target="tpu_custom_call" | custom-call | flops 19327352832 | bytes 48234496 | tf_op jit(solution)/shard_map/pallas_call | solution.py:32
  161.5 0.5 collective-permute-start.8
  162.0 31.1 %shard_map.167 = (bf16[512,2048]{1,0:T(8,128)(2,1)}, bf16[512,2048]{1,0:T(8,128)(2,1)}, bf16[512,2048]{1,0:T(8,128)(2,1)}, bf16[256,3072]{1,0:T(8,128)(2,1)}, bf16[256,3072]{1,0:T(8,128)(2,1)}) custom-call(s32[4]{0:T(128)} %iota_xor_fusion.refs_0_, bf16[256,3072]{1,0:T(8,128)(2,1)} %collective-permute-done.2.refs_1_.refs_7_, ...), custom_call_target="tpu_custom_call" | custom-call | flops 19327352832 | bytes 48234496 | tf_op jit(solution)/shard_map/pallas_call | solution.py:32
  193.1 0.1 collective-permute-start.6
  193.1 0.5 collective-permute-start.10
  193.6 0.0 collective-permute-start.1
  193.6 0.5 collective-permute-start.12
  194.1 3.6 add_convert_fusion.refs_9_
  197.7 2.0 collective-permute-start.9
  199.7 1.8 add_convert_fusion.1.refs_11_
  201.5 34.8 %shard_map.168.refs_10_ = f32[2048,3072]{1,0:T(8,128)} custom-call(bf16[1024,2048]{1,0:T(8,128)(2,1)} %get-tuple-element.45.refs_0_, bf16[512,2048]{1,0:T(8,128)(2,1)} %get-tuple-element.46.refs_1_, bf16[512,2048]{1,0:T(8,128)(2,1)} %get-tuple-element.47.refs_2_, bf16[512,3072]{1,0:T(8,128)(2,1)} %refs_3_.9, ...), custom_call_target="tpu_custom_call" | custom-call | flops 25769803776 | bytes 25165824 | tf_op jit(solution)/shard_map/pallas_call | solution.py:32
  236.3 23.5 %shard_map.169 = (f32[3072,2048]{1,0:T(8,128)}, f32[3072,2048]{1,0:T(8,128)}) custom-call(bf16[512,3072]{1,0:T(8,128)(2,1)} %refs_0_.9, bf16[512,3072]{1,0:T(8,128)(2,1)} %collective-permute-done.10.refs_1_, bf16[512,3072]{1,0:T(8,128)(2,1)} %collective-permute-done.11.refs_2_, bf16[512,3072]{1,0:T(8,128)(2,1)} %collective-permute-done.12.refs_3_, ...), custom_call_target="tpu_custom_call" | custom-call | flops 17179869184 | bytes 16777216 | tf_op jit(solution)/shard_map/pallas_call | solution.py:32
  259.8 6.6 %shard_map.170 = (bf16[256,3072]{1,0:T(8,128)(2,1)}, bf16[512,3072]{1,0:T(8,128)(2,1)}) custom-call(bf16[512,3072]{1,0:T(8,128)(2,1)} %get-tuple-element.33.refs_10_.refs_0_, bf16[512,3072]{1,0:T(8,128)(2,1)} %collective-permute-done.1.refs_1_, bf16[256,3072]{1,0:T(8,128)(2,1)} %collective-permute-done.9.refs_2_, bf16[512,3072]{1,0:T(8,128)(2,1)} %refs_3_.11, ...), custom_call_target="tpu_custom_call" | custom-call | flops 15728640 | bytes 11010048 | tf_op jit(solution)/shard_map/pallas_call | solution.py:32
  266.5 23.7 %shard_map.171 = (f32[3072,2048]{1,0:T(8,128)}, f32[3072,2048]{1,0:T(8,128)}) custom-call(bf16[512,3072]{1,0:T(8,128)(2,1)} %refs_0_.9, bf16[512,3072]{1,0:T(8,128)(2,1)} %collective-permute-done.10.refs_1_, bf16[512,3072]{1,0:T(8,128)(2,1)} %collective-permute-done.11.refs_2_, ...), custom_call_target="tpu_custom_call", output_to_operand_aliasing={{0}: (10, {}), {1}: (11, {})} | custom-call | flops 17179869184 | bytes 16777216 | tf_op jit(solution)/shard_map/pallas_call | solution.py:32
  290.2 6.9 %shard_map.172 = (bf16[256,3072]{1,0:T(8,128)(2,1)}, bf16[512,3072]{1,0:T(8,128)(2,1)}) custom-call(bf16[512,3072]{1,0:T(8,128)(2,1)} %get-tuple-element.33.refs_10_.refs_0_, bf16[512,3072]{1,0:T(8,128)(2,1)} %collective-permute-done.1.refs_1_, bf16[256,3072]{1,0:T(8,128)(2,1)} %collective-permute-done.7.refs_2_, ...), custom_call_target="tpu_custom_call", output_to_operand_aliasing={{1}: (6, {})} | custom-call | flops 15728640 | bytes 11010048 | tf_op jit(solution)/shard_map/pallas_call | solution.py:32
  297.1 2.0 collective-permute-start.17
  299.1 0.5 collective-permute-start.13
  299.6 35.0 %collective-permute-done.17.refs_6_ = bf16[256,3072]{1,0:T(8,128)(2,1)} collective-permute-done((bf16[256,3072]{1,0:T(8,128)(2,1)}, bf16[256,3072]{1,0:T(8,128)(2,1)}, u32[]{:S(2)}, u32[]{:S(2)}) %collective-permute-start.17) | collective-permute-done | bytes 1572896 | tf_op jit(solution)/shard_map/ppermute | solution.py:300
  334.7 32.5 %collective-permute-done.15.refs_5_.refs_4_ = bf16[256,3072]{1,0:T(8,128)(2,1)} collective-permute-done((bf16[256,3072]{1,0:T(8,128)(2,1)}, bf16[256,3072]{1,0:T(8,128)(2,1)}, u32[]{:S(2)}, u32[]{:S(2)}) %collective-permute-start.15) | collective-permute-done | bytes 1572896 | tf_op jit(solution)/shard_map/ppermute | solution.py:300
  367.2 23.5 %shard_map.173 = (f32[3072,2048]{1,0:T(8,128)}, f32[3072,2048]{1,0:T(8,128)}) custom-call(bf16[512,3072]{1,0:T(8,128)(2,1)} %refs_0_.9, bf16[512,3072]{1,0:T(8,128)(2,1)} %collective-permute-done.10.refs_1_, bf16[512,3072]{1,0:T(8,128)(2,1)} %collective-permute-done.11.refs_2_, ...), custom_call_target="tpu_custom_call", output_to_operand_aliasing={{0}: (10, {}), {1}: (11, {})} | custom-call | flops 17179869184 | bytes 16777216 | tf_op jit(solution)/shard_map/pallas_call | solution.py:32
  390.7 15.7 %shard_map.174.refs_16_ = bf16[2048,768]{1,0:T(8,128)(2,1)} custom-call(s32[4]{0:T(128)} %iota_xor_fusion.refs_0_, bf16[512,3072]{1,0:T(8,128)(2,1)} %get-tuple-element.27.refs_1_.refs_2_, bf16[512,3072]{1,0:T(8,128)(2,1)} %get-tuple-element.27.refs_1_.refs_2_, bf16[256,3072]{1,0:T(8,128)(2,1)} %collective-permute-done.13.refs_3_.refs_2_, ...), custom_call_target="tpu_custom_call" | custom-call | flops 7247757312 | bytes 4718592 | tf_op jit(solution)/shard_map/pallas_call | solution.py:32
  406.4 20.4 %shard_map.175 = (bf16[2048,768]{1,0:T(8,128)(2,1)}, f32[768,3072]{1,0:T(8,128)}) custom-call(s32[4]{0:T(128)} %iota_xor_fusion.refs_0_, bf16[512,3072]{1,0:T(8,128)(2,1)} %get-tuple-element.27.refs_1_.refs_2_, bf16[256,3072]{1,0:T(8,128)(2,1)} %collective-permute-done.13.refs_3_.refs_2_, ...), custom_call_target="tpu_custom_call", output_to_operand_aliasing={{0}: (16, {})} | custom-call | flops 12079595520 | bytes 9437184 | tf_op jit(solution)/shard_map/pallas_call | solution.py:32
  (25 shorter events, 0.1 us)
Async XLA Ops:
  0.6 77.3 %collective-permute-start = (bf16[512,3072]{1,0:T(8,128)(2,1)}, bf16[512,3072]{1,0:T(8,128)(2,1)}, u32[]{:S(2)}, u32[]{:S(2)}) collective-permute-start(bf16[512,3072]{1,0:T(8,128)(2,1)} %refs_3_.9), channel_id=1, source_target_pairs={{0,1},{1,0},{2,3},{3,2},{4,5},{5,4},{6,7},{7,6}} | collective-permute-start | bytes 9437192 | tf_op jit(solution)/shard_map/ppermute | solution.py:297
  6.1 38.1 %collective-permute-start.2 = (bf16[256,3072]{1,0:T(8,128)(2,1)}, bf16[256,3072]{1,0:T(8,128)(2,1)}, u32[]{:S(2)}, u32[]{:S(2)}) collective-permute-start(bf16[256,3072]{1,0:T(8,128)(2,1)} %shard_map.164.refs_11_), channel_id=1, source_target_pairs={{0,2},{1,3},{2,0},{3,1},{4,6},{5,7},{6,4},{7,5}} | collective-permute-start | bytes 4718600 | tf_op jit(solution)/shard_map/ppermute | solution.py:300
  8.6 69.3 %collective-permute-start.4 = (bf16[256,3072]{1,0:T(8,128)(2,1)}, bf16[256,3072]{1,0:T(8,128)(2,1)}, u32[]{:S(2)}, u32[]{:S(2)}) collective-permute-start(bf16[256,3072]{1,0:T(8,128)(2,1)} %shard_map.163.refs_1_), channel_id=1, source_target_pairs={{0,2},{1,3},{2,0},{3,1},{4,6},{5,7},{6,4},{7,5}} | collective-permute-start | bytes 4718600 | tf_op jit(solution)/shard_map/ppermute | solution.py:300
  8.7 185.0 %collective-permute-start.11 = (bf16[512,3072]{1,0:T(8,128)(2,1)}, bf16[512,3072]{1,0:T(8,128)(2,1)}, u32[]{:S(2)}, u32[]{:S(2)}) collective-permute-start(bf16[512,3072]{1,0:T(8,128)(2,1)} %refs_0_.9), channel_id=1, source_target_pairs={{0,2},{1,3},{2,0},{3,1},{4,6},{5,7},{6,4},{7,5}} | collective-permute-start | bytes 9437192 | tf_op jit(solution)/shard_map/ppermute | solution.py:300
  44.2 117.8 %collective-permute-start.3 = (bf16[256,3072]{1,0:T(8,128)(2,1)}, bf16[256,3072]{1,0:T(8,128)(2,1)}, u32[]{:S(2)}, u32[]{:S(2)}) collective-permute-start(bf16[256,3072]{1,0:T(8,128)(2,1)} %collective-permute-done.2.refs_1_.refs_7_), channel_id=1, source_target_pairs={{0,1},{1,0},{2,3},{3,2},{4,5},{5,4},{6,7},{7,6}} | collective-permute-start | bytes 4718600 | tf_op jit(solution)/shard_map/ppermute | solution.py:297
  77.9 52.7 %collective-permute-start.5 = (bf16[256,3072]{1,0:T(8,128)(2,1)}, bf16[256,3072]{1,0:T(8,128)(2,1)}, u32[]{:S(2)}, u32[]{:S(2)}) collective-permute-start(bf16[256,3072]{1,0:T(8,128)(2,1)} %collective-permute-done.4.refs_1_.refs_5_), channel_id=1, source_target_pairs={{0,1},{1,0},{2,3},{3,2},{4,5},{5,4},{6,7},{7,6}} | collective-permute-start | bytes 4718600 | tf_op jit(solution)/shard_map/ppermute | solution.py:297
  161.5 32.7 %collective-permute-start.8 = (bf16[256,3072]{1,0:T(8,128)(2,1)}, bf16[256,3072]{1,0:T(8,128)(2,1)}, u32[]{:S(2)}, u32[]{:S(2)}) collective-permute-start(bf16[256,3072]{1,0:T(8,128)(2,1)} %get-tuple-element.38), channel_id=1, source_target_pairs={{0,1},{1,0},{2,3},{3,2},{4,5},{5,4},{6,7},{7,6}} | collective-permute-start | bytes 4718600 | tf_op jit(solution)/shard_map/ppermute | solution.py:297
  193.1 6.7 %copy-start = (bf16[256,3072]{1,0:T(8,128)(2,1)S(1)}, bf16[256,3072]{1,0:T(8,128)(2,1)}, u32[]{:S(2)}) copy-start(bf16[256,3072]{1,0:T(8,128)(2,1)} %get-tuple-element.36) | copy-start | bytes 4718596
  193.1 6.7 %collective-permute-start.6 = (bf16[256,3072]{1,0:T(8,128)(2,1)}, bf16[256,3072]{1,0:T(8,128)(2,1)S(1)}, u32[]{:S(2)}, u32[]{:S(2)}) collective-permute-start(bf16[256,3072]{1,0:T(8,128)(2,1)} %get-tuple-element.37), channel_id=1, source_target_pairs={{0,1},{1,0},{2,3},{3,2},{4,5},{5,4},{6,7},{7,6}} | collective-permute-start | bytes 4718600 | tf_op jit(solution)/shard_map/ppermute | solution.py:297
  193.1 43.2 %collective-permute-start.10 = (bf16[512,3072]{1,0:T(8,128)(2,1)}, bf16[512,3072]{1,0:T(8,128)(2,1)}, u32[]{:S(2)}, u32[]{:S(2)}) collective-permute-start(bf16[512,3072]{1,0:T(8,128)(2,1)} %refs_0_.9), channel_id=1, source_target_pairs={{0,1},{1,0},{2,3},{3,2},{4,5},{5,4},{6,7},{7,6}} | collective-permute-start | bytes 9437192 | tf_op jit(solution)/shard_map/ppermute | solution.py:297
  193.6 66.2 %collective-permute-start.1 = (bf16[512,3072]{1,0:T(8,128)(2,1)}, bf16[512,3072]{1,0:T(8,128)(2,1)}, u32[]{:S(2)}, u32[]{:S(2)}) collective-permute-start(bf16[512,3072]{1,0:T(8,128)(2,1)} %get-tuple-element.34), channel_id=1, source_target_pairs={{0,1},{1,0},{2,3},{3,2},{4,5},{5,4},{6,7},{7,6}} | collective-permute-start | bytes 9437192 | tf_op jit(solution)/shard_map/ppermute | solution.py:297
  193.6 42.7 %collective-permute-start.12 = (bf16[512,3072]{1,0:T(8,128)(2,1)}, bf16[512,3072]{1,0:T(8,128)(2,1)}, u32[]{:S(2)}, u32[]{:S(2)}) collective-permute-start(bf16[512,3072]{1,0:T(8,128)(2,1)} %collective-permute-done.11.refs_2_), channel_id=1, source_target_pairs={{0,1},{1,0},{2,3},{3,2},{4,5},{5,4},{6,7},{7,6}} | collective-permute-start | bytes 9437192 | tf_op jit(solution)/shard_map/ppermute | solution.py:297
  197.7 62.1 %collective-permute-start.9 = (bf16[256,3072]{1,0:T(8,128)(2,1)}, bf16[256,3072]{1,0:T(8,128)(2,1)}, u32[]{:S(2)}, u32[]{:S(2)}) collective-permute-start(bf16[256,3072]{1,0:T(8,128)(2,1)} %add_convert_fusion.refs_9_), channel_id=1, source_target_pairs={{0,2},{1,3},{2,0},{3,1},{4,6},{5,7},{6,4},{7,5}} | collective-permute-start | bytes 4718600 | tf_op jit(solution)/shard_map/ppermute | solution.py:300
  201.5 88.7 %collective-permute-start.7 = (bf16[256,3072]{1,0:T(8,128)(2,1)}, bf16[256,3072]{1,0:T(8,128)(2,1)}, u32[]{:S(2)}, u32[]{:S(2)}) collective-permute-start(bf16[256,3072]{1,0:T(8,128)(2,1)} %add_convert_fusion.1.refs_11_), channel_id=1, source_target_pairs={{0,2},{1,3},{2,0},{3,1},{4,6},{5,7},{6,4},{7,5}} | collective-permute-start | bytes 4718600 | tf_op jit(solution)/shard_map/ppermute | solution.py:300
  297.1 37.6 %collective-permute-start.17 = (bf16[256,3072]{1,0:T(8,128)(2,1)}, bf16[256,3072]{1,0:T(8,128)(2,1)}, u32[]{:S(2)}, u32[]{:S(2)}) collective-permute-start(bf16[256,3072]{1,0:T(8,128)(2,1)} %get-tuple-element.54.refs_12_), channel_id=1, source_target_pairs={{0,2},{1,3},{2,0},{3,1},{4,6},{5,7},{6,4},{7,5}} | collective-permute-start | bytes 4718600 | tf_op jit(solution)/shard_map/ppermute | solution.py:300
  299.1 68.1 %collective-permute-start.15 = (bf16[256,3072]{1,0:T(8,128)(2,1)}, bf16[256,3072]{1,0:T(8,128)(2,1)}, u32[]{:S(2)}, u32[]{:S(2)}) collective-permute-start(bf16[256,3072]{1,0:T(8,128)(2,1)} %get-tuple-element.51.refs_12_), channel_id=1, source_target_pairs={{0,2},{1,3},{2,0},{3,1},{4,6},{5,7},{6,4},{7,5}} | collective-permute-start | bytes 4718600 | tf_op jit(solution)/shard_map/ppermute | solution.py:300
  299.1 91.5 %collective-permute-start.14 = (bf16[256,3072]{1,0:T(8,128)(2,1)}, bf16[256,3072]{1,0:T(8,128)(2,1)}, u32[]{:S(2)}, u32[]{:S(2)}) collective-permute-start(bf16[256,3072]{1,0:T(8,128)(2,1)} %get-tuple-element.54.refs_12_), channel_id=1, source_target_pairs={{0,1},{1,0},{2,3},{3,2},{4,5},{5,4},{6,7},{7,6}} | collective-permute-start | bytes 4718600 | tf_op jit(solution)/shard_map/ppermute | solution.py:297
  299.1 91.5 %collective-permute-start.13 = (bf16[256,3072]{1,0:T(8,128)(2,1)}, bf16[256,3072]{1,0:T(8,128)(2,1)}, u32[]{:S(2)}, u32[]{:S(2)}) collective-permute-start(bf16[256,3072]{1,0:T(8,128)(2,1)} %get-tuple-element.51.refs_12_), channel_id=1, source_target_pairs={{0,1},{1,0},{2,3},{3,2},{4,5},{5,4},{6,7},{7,6}} | collective-permute-start | bytes 4718600 | tf_op jit(solution)/shard_map/ppermute | solution.py:297
  334.7 71.7 %collective-permute-start.18 = (bf16[256,3072]{1,0:T(8,128)(2,1)}, bf16[256,3072]{1,0:T(8,128)(2,1)}, u32[]{:S(2)}, u32[]{:S(2)}) collective-permute-start(bf16[256,3072]{1,0:T(8,128)(2,1)} %collective-permute-done.17.refs_6_), channel_id=1, source_target_pairs={{0,1},{1,0},{2,3},{3,2},{4,5},{5,4},{6,7},{7,6}} | collective-permute-start | bytes 4718600 | tf_op jit(solution)/shard_map/ppermute | solution.py:297
  367.2 23.5 %collective-permute-start.16 = (bf16[256,3072]{1,0:T(8,128)(2,1)}, bf16[256,3072]{1,0:T(8,128)(2,1)}, u32[]{:S(2)}, u32[]{:S(2)}) collective-permute-start(bf16[256,3072]{1,0:T(8,128)(2,1)} %collective-permute-done.15.refs_5_.refs_4_), channel_id=1, source_target_pairs={{0,1},{1,0},{2,3},{3,2},{4,5},{5,4},{6,7},{7,6}} | collective-permute-start | bytes 4718600 | tf_op jit(solution)/shard_map/ppermute | solution.py:297

commit v2 on v1

--- a/solution.py
+++ b/solution.py
@@ -49,17 +49,34 @@
     return run
 
 
-def input_grads(pieces, starts, w_down, w_gate, w_up, u_gate, u_up, offs, cols, x_cols, after=()):
+def input_grads(pieces, starts, w_down, w_gate, w_up, u_gate, u_up, offs, cols, x_cols, terms=(), after=()):
     rows, width = pieces[0].shape
     n_cols = w_down.shape[0]
     total = 2 * rows
     n_gate, n_x = n_cols // cols, width // x_cols
 
-    def kernel(y0, y1, wd, g0, g1, u0, u1, wg, wu, o_gate, o_up, o_z, o_x0, o_x1, s_gate, s_up):
+    def kernel(y0, y1, wd, g0, g1, u0, u1, wg, wu, *refs):
+        o_gate, o_up, o_z, o_x0, o_x1 = refs[len(terms):len(terms) + 5]
+        s_gate, s_up, held, sem = refs[-4:]
         step = pl.program_id(0)
 
+        def fetch(tile):
+            at = pl.ds(pl.multiple_of(tile * x_cols, x_cols), x_cols)
+            slot = lax.rem(tile, 2)
+            return [pltpu.make_async_copy(w.at[at], held.at[slot, k], sem.at[slot, k]) for k, w in enumerate((wg, wu))]
+
+        @pl.when(step == n_gate - 1)
+        def _():
+            for copy in fetch(0):
+                copy.start()
+
+        def add_terms():
+            if terms:
+                refs[7][...] = (refs[0][...].astype(F32) + refs[1][...].astype(F32)).astype(BF16)
+
         @pl.when(step < n_gate)
         def _():
+            add_terms()
             at = pl.ds(pl.multiple_of(step * cols, cols), cols)
             grad_y = jnp.concatenate([y0[...], y1[...]], axis=0)
             grad_h = lax.dot_general(grad_y, wd[...], NT, preferred_element_type=F32)
@@ -77,8 +94,19 @@
 
         @pl.when(step >= n_gate)
         def _():
-            part = (lax.dot_general(s_gate[...], wg[...], NT, preferred_element_type=F32)
-                    + lax.dot_general(s_up[...], wu[...], NT, preferred_element_type=F32)).astype(BF16)
+            tile = step - n_gate
+
+            @pl.when(tile + 1 < n_x)
+            def _():
+                for copy in fetch(tile + 1):
+                    copy.start()
+
+            for copy in fetch(tile):
+                copy.wait()
+            add_terms()
+            slot = lax.rem(tile, 2)
+            part = (lax.dot_general(s_gate[...], held[slot, 0], NT, preferred_element_type=F32)
+                    + lax.dot_general(s_up[...], held[slot, 1], NT, preferred_element_type=F32)).astype(BF16)
             o_x0[...] = part[:rows]
             o_x1[...] = part[rows:]
 
@@ -86,20 +114,23 @@
     second = lambda j: jnp.maximum(j - n_gate, 0)
     whole = pl.BlockSpec((rows, width), lambda j, o: (0, 0))
     tiles = [pl.BlockSpec((rows, cols), functools.partial(lambda s, j, o: (s(o), first(j)), s)) for s in starts]
-    w_x = pl.BlockSpec((x_cols, n_cols), lambda j, o: (second(j), 0))
+    w_x = pl.BlockSpec(memory_space=pl.ANY)
     out = pl.BlockSpec((total, cols), lambda j, o: (0, first(j)))
     out_x = pl.BlockSpec((rows, x_cols), lambda j, o: (0, second(j)))
+    sums = [pl.BlockSpec((t.shape[0] // 8, width), lambda j, o: (jnp.minimum(j, 7), 0)) for t in terms]
     return call(
         kernel, (n_gate + n_x,),
-        [whole, whole, pl.BlockSpec((cols, width), lambda j, o: (first(j), 0)), *tiles, *tiles, w_x, w_x],
-        [out] * 3 + [out_x] * 2,
-        [jax.ShapeDtypeStruct((total, n_cols), BF16)] * 3 + [jax.ShapeDtypeStruct((rows, width), BF16)] * 2,
+        [whole, whole, pl.BlockSpec((cols, width), lambda j, o: (first(j), 0)), *tiles, *tiles, w_x, w_x, *sums],
+        [out] * 3 + [out_x] * 2 + sums[:1],
+        [jax.ShapeDtypeStruct((total, n_cols), BF16)] * 3 + [jax.ShapeDtypeStruct((rows, width), BF16)] * 2
+        + [jax.ShapeDtypeStruct(t.shape, BF16) for t in terms[:1]],
         6 * total * width * n_cols, 2 * n_cols * (3 * width + 5 * total),
-        scratch=[pltpu.VMEM((total, n_cols), BF16)] * 2, after=after, offs=offs,
-    )(*pieces, w_down, u_gate, u_gate, u_up, u_up, w_gate, w_up)
-
-
-def gw_in(x_parts, gates, ups, span, prev, rows, cols, after=()):
+        scratch=[pltpu.VMEM((total, n_cols), BF16)] * 2
+        + [pltpu.VMEM((2, 2, x_cols, n_cols), BF16), pltpu.SemaphoreType.DMA((2, 2))], after=after, offs=offs,
+    )(*pieces, w_down, u_gate, u_gate, u_up, u_up, w_gate, w_up, *terms)
+
+
+def gw_in(x_parts, gates, ups, span, prev, rows, cols, norm=(), norm_size=0, after=()):
     width = x_parts[0].shape[1]
     n_tok = sum(x.shape[0] for x in x_parts)
     n_cols = gates[0].shape[1]
@@ -116,6 +147,10 @@
                 term = lax.dot_general(a, d[...], TN, preferred_element_type=F32)
                 total = term if total is None else total + term
             out[...] = total
+        if norm:
+            some = norm_rows(*refs[10:16])
+            refs[16][...] = some
+            refs[17][...] = some
 
     in_specs = [pl.BlockSpec((x.shape[0], rows), lambda i, j: (0, start + i)) for x in x_parts]
     in_specs += [pl.BlockSpec((d.shape[0], cols), lambda i, j: (0, j)) for d in (*gates, *ups)]
@@ -125,10 +160,17 @@
         in_specs += [pl.BlockSpec(memory_space=pl.ANY)] * 2
         args += list(prev)
         aliases = {10: 0, 11: 1}
+    more_specs, more = [], []
+    if norm:
+        some_rows = pl.BlockSpec((norm_size * cols // n_cols, width), lambda i, j: (j, 0))
+        in_specs += [some_rows] * 4 + [pl.BlockSpec((width,), lambda i, j: (0,)), some_rows]
+        args += list(norm)
+        more_specs = [some_rows] * 2
+        more = [jax.ShapeDtypeStruct((norm_size, width), BF16), jax.ShapeDtypeStruct(norm[3].shape, BF16)]
     return call(
         kernel, (count, n_cols // cols), in_specs,
-        [pl.BlockSpec((rows, cols), lambda i, j: (start + i, j))] * 2,
-        [jax.ShapeDtypeStruct((width, n_cols), F32)] * 2,
+        more_specs + [pl.BlockSpec((rows, cols), lambda i, j: (start + i, j))] * 2,
+        more + [jax.ShapeDtypeStruct((width, n_cols), F32)] * 2,
         4 * n_tok * (span[1] - span[0]) * n_cols, 8 * (span[1] - span[0]) * n_cols, after=after, aliases=aliases,
     )(*args)
 
@@ -171,6 +213,15 @@
     )(x)
 
 
+def norm_rows(p0, p1, p2, x_in, gamma, grad_res):
+    grad_x = (p0[...].astype(F32) + p1[...].astype(F32) + p2[...].astype(F32)).astype(BF16).astype(F32)
+    xin_f = x_in[...].astype(F32)
+    inv_rms = lax.rsqrt(jnp.mean(xin_f * xin_f, axis=-1, keepdims=True) + NORM_EPS)
+    scaled = grad_x * gamma[...].astype(F32).reshape(1, -1)
+    proj_mean = jnp.mean(scaled * xin_f, axis=-1, keepdims=True)
+    return (grad_res[...].astype(F32) + inv_rms * (scaled - xin_f * (inv_rms * inv_rms) * proj_mean)).astype(BF16)
+
+
 def norm_chunk(parts, starts, rows, first_row, x_in, gamma, grad_res, prev, cuts, block=128, after=()):
     width = x_in.shape[1]
     n_cuts = len(cuts)
@@ -178,12 +229,7 @@
 
     def kernel(p0, p1, p2, xin, gam, res, *outs):
         outs = outs[-1 - n_cuts:]
-        grad_x = (p0[...].astype(F32) + p1[...].astype(F32) + p2[...].astype(F32)).astype(BF16).astype(F32)
-        xin_f = xin[...].astype(F32)
-        inv_rms = lax.rsqrt(jnp.mean(xin_f * xin_f, axis=-1, keepdims=True) + NORM_EPS)
-        scaled = grad_x * gam[...].astype(F32)
-        proj_mean = jnp.mean(scaled * xin_f, axis=-1, keepdims=True)
-        out = (res[...].astype(F32) + inv_rms * (scaled - xin_f * (inv_rms * inv_rms) * proj_mean)).astype(BF16)
+        out = norm_rows(p0, p1, p2, xin, gam, res)
         outs[-1][...] = out
         for k in range(n_cuts):
             @pl.when((pl.program_id(0) >= edges[k]) & (pl.program_id(0) < edges[k + 1]))
@@ -193,7 +239,7 @@
     first = first_row // block
     at = lambda s: pl.BlockSpec((block, width), lambda i: (s + i, 0))
     cut = lambda k: pl.BlockSpec((block, width), lambda i: (jnp.clip(i - edges[k], 0, edges[k + 1] - edges[k] - 1), 0))
-    in_specs = [at(s // block) for s in starts] + [at(first), pl.BlockSpec((1, width), lambda i: (0, 0)), at(first)]
+    in_specs = [at(s // block) for s in starts] + [at(first), pl.BlockSpec((width,), lambda i: (0,)), at(first)]
     args = [*parts, x_in, gamma, grad_res]
     aliases = None
     if prev is not None:
@@ -207,30 +253,41 @@
     )(*args)
 
 
-def grad_attention(pieces, at_rows, blocks, w_out, offs, n_tok, after=()):
+def grad_attention(pieces, at_rows, blocks, w_out, offs, n_tok, group=2, after=()):
     n_cols, width = w_out.shape
     n = len(pieces)
     size = n_tok // 8
 
-    def kernel(*refs):
-        srcs, w, out = refs[:n], refs[n], refs[-1]
-        for q in range(n):
-            @pl.when(pl.program_id(0) == q)
-            def _(q=q):
-                out[...] = lax.dot_general(srcs[q][...], w[...], NT, preferred_element_type=F32).astype(BF16)
-
-    def out_map(j, o):
-        row = blocks[0](o)
-        for q in range(1, n):
-            row = jnp.where(j >= q, blocks[q](o), row)
-        return (row, 0)
-
-    return call(
-        kernel, (n,),
-        [pl.BlockSpec((size, width), functools.partial(lambda r, j, o: (r, 0), r)) for r in at_rows]
-        + [pl.BlockSpec((n_cols, width), lambda j, o: (0, 0))],
-        pl.BlockSpec((size, n_cols), out_map), jax.ShapeDtypeStruct((n_tok, n_cols), BF16),
-        2 * n * size * width * n_cols, 2 * width * n_cols, after=after, offs=offs,
+    def kernel(offs_ref, *refs):
+        srcs, w, out, held, held_w, made, in_sem, w_sem, out_sem = *(refs[:n],), *refs[n:]
+        loads = [pltpu.make_async_copy(w, held_w, w_sem.at[0])]
+        loads += [pltpu.make_async_copy(srcs[q].at[pl.ds(at_rows[q] * size, size)], held.at[q], in_sem.at[q]) for q in range(n)]
+        for load in loads[:1 + group]:
+            load.start()
+        loads[0].wait()
+        stores = []
+        for first in range(0, n, group):
+            for q in range(first, first + group):
+                loads[1 + q].wait()
+            if first == 0:
+                for load in loads[1 + group:]:
+                    load.start()
+            lhs = held[first:first + group].reshape(group * size, width)
+            part = lax.dot_general(lhs, held_w[...], NT, preferred_element_type=F32).astype(BF16)
+            made[first:first + group] = part.reshape(group, size, n_cols)
+            for q in range(first, first + group):
+                row = pl.multiple_of(blocks[q](offs_ref) * size, size)
+                stores.append(pltpu.make_async_copy(made.at[q], out.at[pl.ds(row, size)], out_sem.at[q]))
+                stores[-1].start()
+        for store in stores:
+            store.wait()
+
+    anywhere = pl.BlockSpec(memory_space=pl.ANY)
+    return call(
+        kernel, (1,), [anywhere] * (n + 1), anywhere, jax.ShapeDtypeStruct((n_tok, n_cols), BF16),
+        2 * n * size * width * n_cols, 2 * width * n_cols, after=after, offs=offs, keep_offs=True,
+        scratch=[pltpu.VMEM((n, size, width), BF16), pltpu.VMEM((n_cols, width), BF16), pltpu.VMEM((n, size, n_cols), BF16),
+                 pltpu.SemaphoreType.DMA((n,)), pltpu.SemaphoreType.DMA((1,)), pltpu.SemaphoreType.DMA((n,))],
     )(*pieces, w_out)
 
 
@@ -304,7 +361,7 @@
         half = own // 2
         n_tok = u_gate.shape[0]
         offs = lax.axis_index("tp") ^ jnp.arange(4, dtype=jnp.int32)
-        gain = gamma.reshape(1, width)
+        gain = gamma
         of = lambda p, c: (lambda o: 2 * o[p] + c)
         weights = (w_down, w_gate, w_up, u_gate, u_up, offs)
 
@@ -319,26 +376,26 @@
         x_parts = (x_norm, x_par, x_acr, x_dia)
 
         g_l, u_l, z_l, dx_own, dx_par = input_grads(
-            (grad_y, y_par), (lambda o: o[0], lambda o: o[1]), *weights, 256, 512, after=(gain, head1))
+            (grad_y, y_par), (lambda o: o[0], lambda o: o[1]), *weights, 256, 512, after=(head1,))
         dx_sib = swap(dx_par)
-        gates, ups, zs, dx_rem = [g_l], [u_l], [z_l], []
-        last = dx_own
+        gates, ups, zs = [g_l], [u_l], [z_l]
+        last, terms, both = dx_own, (), []
         for c in range(2):
-            g, u, z, to_acr, to_dia = input_grads(
-                (y_acr[c], y_dia[c]), (of(2, c), of(3, c)), *weights, 512, 512, after=(last,))
-            dx_rem.append((to_acr, swap(to_dia)))
-            last = to_acr
+            g, u, z, to_acr, to_dia, *summed = input_grads(
+                (y_acr[c], y_dia[c]), (of(2, c), of(3, c)), *weights, 512, 512, terms=terms, after=(last,))
+            both += summed
+            last, terms = to_acr, (to_acr, swap(to_dia))
             gates.append(g)
             ups.append(u)
             zs.append(z)
-        both = [(a.astype(F32) + b.astype(F32)).astype(BF16) for a, b in dx_rem]
+        both.append((terms[0].astype(F32) + terms[1].astype(F32)).astype(BF16))
         rs = [send(both[c]) for c in range(2)]
 
-        gwd = gw_down(zs, ((grad_y, y_par), (y_acr[0], y_dia[0]), (y_acr[1], y_dia[1])), 1024, 512, after=(both[0],))
+        gwd = gw_down(zs, ((grad_y, y_par), (y_acr[0], y_dia[0]), (y_acr[1], y_dia[1])), 1024, 1024, after=(last,))
         third = width // 3
         norm = (x_in, gain, grad_res)
-        gw = gw_in(x_parts, gates, ups, (0, third), None, 1024, 512, after=(gwd, both[1]))
-        ds0, ds = norm_chunk((dx_own, dx_sib, rs[0]), (0, 0, 0), half, 0, *norm, None, (half,), after=(gw[0],))
+        ds0, ds, *gw = gw_in(x_parts, gates, ups, (0, third), None, 1024, 512,
+                             norm=(dx_own, dx_sib, rs[0], *norm), norm_size=half, after=(gwd, both[1]))
         s_acr0, s_par0 = send(ds0), swap(ds0)
         gw = gw_in(x_parts, gates, ups, (third, 2 * third), gw, 1024, 512, after=(ds0,))
         ds1, ds = norm_chunk((dx_own, dx_sib, rs[1]), (half, half, 0), half, half, *norm, ds, (half,), after=(gw[0],))

time: 427 us -> 395 us (0.925)
  waiting for transfers between devices: 133 us -> 111 us
  Pallas kernels: 274 us -> 268 us
    ppermute x7, waiting for transfers between devices: 133 us -> 108 us  [send(): return lax.ppermute(x, 'tp', across)]
    pallas_call x13 -> x12, Pallas kernels: 274 us -> 268 us  [launch(): pl.pallas_call(body, grid_spec=pltpu.PrefetchScalarGridSpec(num_scalar_pr...]
  transfers between devices with their start and end apart: 19 -> 19, of which waited for: 4 -> 5; matrix products, arithmetic and copies ran while one was open for 2% -> 1% of each run, Pallas kernels for 58% -> 63%
where the time goes in v2:
time: 395 us
  Pallas kernels  268 us (68%)
  waiting for transfers between devices  111 us (28%)
  starting transfers between devices  11.5 us (3%)
  other arithmetic  4.08 us (1%)
    pallas_call x12, Pallas kernels, launch(): pl.pallas_call(body, grid_spec=pltpu.PrefetchScalarGridSpec(num_scalar_pr...  268 us
    ppermute x7, waiting for transfers between devices, send(): return lax.ppermute(x, 'tp', across)  108 us
    ppermute x7, starting transfers between devices, send(): return lax.ppermute(x, 'tp', across)  8.63 us
  transfers between devices with their start and end apart: 19, of which 5 were waited for; matrix products, arithmetic and copies ran while one was open for 1% of the time, Pallas kernels for 63%

profile of v2, /device:TPU:0, one launch (start us, length us, event | category | flops | bytes accessed | tf_op | source)
XLA Modules:
  0.0 394.9 jit_solution(17996119169770119864)
XLA Ops:
  0.6 0.9 collective-permute-start
  1.5 2.3 shard_map.163.refs_1_
  3.8 2.5 collective-permute-start.4
  6.3 2.3 shard_map.164.refs_10_
  8.6 2.0 collective-permute-start.10
  10.7 0.5 iota_xor_fusion.refs_0_
  11.1 30.7 %collective-permute-done.4.refs_1_.refs_5_ = bf16[256,3072]{1,0:T(8,128)(2,1)} collective-permute-done((bf16[256,3072]{1,0:T(8,128)(2,1)}, bf16[256,3072]{1,0:T(8,128)(2,1)}, u32[]{:S(2)}, u32[]{:S(2)}) %collective-permute-start.4) | collective-permute-done | bytes 1572896 | tf_op jit(solution)/shard_map/ppermute | solution.py:357
  41.9 33.7 %collective-permute-done.2.refs_1_.refs_7_ = bf16[256,3072]{1,0:T(8,128)(2,1)} collective-permute-done((bf16[256,3072]{1,0:T(8,128)(2,1)}, bf16[256,3072]{1,0:T(8,128)(2,1)}, u32[]{:S(2)}, u32[]{:S(2)}) %collective-permute-start.2) | collective-permute-done | bytes 1572896 | tf_op jit(solution)/shard_map/ppermute | solution.py:357
  75.6 51.9 %shard_map.165 = (bf16[1024,2048]{1,0:T(8,128)(2,1)}, bf16[1024,2048]{1,0:T(8,128)(2,1)}, bf16[1024,2048]{1,0:T(8,128)(2,1)}, bf16[512,3072]{1,0:T(8,128)(2,1)}, bf16[512,3072]{1,0:T(8,128)(2,1)}) custom-call(s32[4]{0:T(128)} %iota_xor_fusion.refs_0_, bf16[512,3072]{1,0:T(8,128)(2,1)} %refs_3_.8, bf16[512,3072]{1,0:T(8,128)(2,1)} %collective-permute-done.refs_2_.refs_4_, ...), custom_call_target="tpu_custom_call" | custom-call | flops 38654705664 | bytes 58720256 | tf_op jit(solution)/shard_map/pallas_call | solution.py:32
  127.5 30.0 %shard_map.166 = (bf16[512,2048]{1,0:T(8,128)(2,1)}, bf16[512,2048]{1,0:T(8,128)(2,1)}, bf16[512,2048]{1,0:T(8,128)(2,1)}, bf16[256,3072]{1,0:T(8,128)(2,1)}, bf16[256,3072]{1,0:T(8,128)(2,1)}) custom-call(s32[4]{0:T(128)} %iota_xor_fusion.refs_0_, bf16[256,3072]{1,0:T(8,128)(2,1)} %collective-permute-done.4.refs_1_.refs_5_, ...), custom_call_target="tpu_custom_call" | custom-call | flops 19327352832 | bytes 48234496 | tf_op jit(solution)/shard_map/pallas_call | solution.py:32
  157.6 0.5 collective-permute-start.6
  158.1 0.0 collective-permute-start.9
  158.1 0.5 collective-permute-start.1
  158.6 0.0 collective-permute-start.11
  158.7 2.8 collective-permute-done.6.refs_11_
  161.5 31.7 %shard_map.167 = (bf16[512,2048]{1,0:T(8,128)(2,1)}, bf16[512,2048]{1,0:T(8,128)(2,1)}, bf16[512,2048]{1,0:T(8,128)(2,1)}, bf16[256,3072]{1,0:T(8,128)(2,1)}, bf...) custom-call(s32[4]{0:T(128)} %iota_xor_fusion.refs_0_, bf16[256,3072]{1,0:T(8,128)(2,1)} %collective-permute-done.2.refs_1_.refs_7_, ...), custom_call_target="tpu_custom_call" | custom-call | flops 19327352832 | bytes 48234496 | tf_op jit(solution)/shard_map/pallas_call | solution.py:32
  193.2 0.4 collective-permute-start.7
  193.6 2.0 collective-permute-start.12
  195.6 33.2 %shard_map.168.refs_16_ = f32[2048,3072]{1,0:T(8,128)} custom-call(bf16[1024,2048]{1,0:T(8,128)(2,1)} %get-tuple-element.47.refs_0_, bf16[512,2048]{1,0:T(8,128)(2,1)} %get-tuple-element.48.refs_1_, bf16[512,2048]{1,0:T(8,128)(2,1)} %get-tuple-element.49.refs_2_, bf16[512,3072]{1,0:T(8,128)(2,1)} %refs_3_.8, ...), custom_call_target="tpu_custom_call" | custom-call | flops 25769803776 | bytes 25165824 | tf_op jit(solution)/shard_map/pallas_call | solution.py:32
  228.9 3.6 add_convert_fusion.refs_17_
  232.5 0.0 collective-permute-start.8
  232.5 27.1 %shard_map.169 = (bf16[256,3072]{1,0:T(8,128)(2,1)}, bf16[512,3072]{1,0:T(8,128)(2,1)}, f32[3072,2048]{1,0:T(8,128)}, f32[3072,2048]{1,0:T(8,128)}) custom-call(bf16[512,3072]{1,0:T(8,128)(2,1)} %refs_0_.9, bf16[512,3072]{1,0:T(8,128)(2,1)} %collective-permute-done.9.refs_1_, bf16[512,3072]{1,0:T(8,128)(2,1)} %collective-permute-done.10.refs_2_, ...), custom_call_target="tpu_custom_call" | custom-call | flops 17179869184 | bytes 16777216 | tf_op jit(solution)/shard_map/pallas_call | solution.py:32
  259.6 2.0 collective-permute-start.15
  261.6 23.7 %shard_map.170 = (f32[3072,2048]{1,0:T(8,128)}, f32[3072,2048]{1,0:T(8,128)}) custom-call(bf16[512,3072]{1,0:T(8,128)(2,1)} %refs_0_.9, bf16[512,3072]{1,0:T(8,128)(2,1)} %collective-permute-done.9.refs_1_, bf16[512,3072]{1,0:T(8,128)(2,1)} %collective-permute-done.10.refs_2_, ...), custom_call_target="tpu_custom_call", output_to_operand_aliasing={{0}: (10, {}), {1}: (11, {})} | custom-call | flops 17179869184 | bytes 16777216 | tf_op jit(solution)/shard_map/pallas_call | solution.py:32
  285.3 6.9 %shard_map.171 = (bf16[256,3072]{1,0:T(8,128)(2,1)}, bf16[512,3072]{1,0:T(8,128)(2,1)}) custom-call(bf16[512,3072]{1,0:T(8,128)(2,1)} %get-tuple-element.34.refs_10_.refs_0_, bf16[512,3072]{1,0:T(8,128)(2,1)} %collective-permute-done.1.refs_11_.refs_1_, bf16[256,3072]{1,0:T(8,128)(2,1)} %collective-permute-done.8.refs_2_, ...), custom_call_target="tpu_custom_call", output_to_operand_aliasing={{1}: (6, {})} | custom-call | flops 15728640 | bytes 11010048 | tf_op jit(solution)/shard_map/pallas_call | solution.py:32
  292.2 0.0 collective-permute-start.17
  292.3 0.5 collective-permute-start.14
  292.8 11.0 %collective-permute-done.15.refs_5_.refs_4_ = bf16[256,3072]{1,0:T(8,128)(2,1)} collective-permute-done((bf16[256,3072]{1,0:T(8,128)(2,1)}, bf16[256,3072]{1,0:T(8,128)(2,1)}, u32[]{:S(2)}, u32[]{:S(2)}) %collective-permute-start.15) | collective-permute-done | bytes 1572896 | tf_op jit(solution)/shard_map/ppermute | solution.py:357
  303.8 32.6 %collective-permute-done.17.refs_6_ = bf16[256,3072]{1,0:T(8,128)(2,1)} collective-permute-done((bf16[256,3072]{1,0:T(8,128)(2,1)}, bf16[256,3072]{1,0:T(8,128)(2,1)}, u32[]{:S(2)}, u32[]{:S(2)}) %collective-permute-start.17) | collective-permute-done | bytes 1572896 | tf_op jit(solution)/shard_map/ppermute | solution.py:357
  336.4 23.5 %shard_map.172 = (f32[3072,2048]{1,0:T(8,128)}, f32[3072,2048]{1,0:T(8,128)}) custom-call(bf16[512,3072]{1,0:T(8,128)(2,1)} %refs_0_.9, bf16[512,3072]{1,0:T(8,128)(2,1)} %collective-permute-done.9.refs_1_, bf16[512,3072]{1,0:T(8,128)(2,1)} %collective-permute-done.10.refs_2_, ...), custom_call_target="tpu_custom_call", output_to_operand_aliasing={{0}: (10, {}), {1}: (11, {})} | custom-call | flops 17179869184 | bytes 16777216 | tf_op jit(solution)/shard_map/pallas_call | solution.py:32
  359.9 14.4 %shard_map.173.refs_16_ = bf16[2048,768]{1,0:T(8,128)(2,1)} custom-call(s32[4]{0:T(128)} %iota_xor_fusion.refs_0_, bf16[512,3072]{1,0:T(8,128)(2,1)} %get-tuple-element.28.refs_1_.refs_2_, bf16[512,3072]{1,0:T(8,128)(2,1)} %get-tuple-element.28.refs_1_.refs_2_, bf16[256,3072]{1,0:T(8,128)(2,1)} %collective-permute-done.13.refs_3_.refs_2_, ...), custom_call_target="tpu_custom_call" | custom-call | flops 7247757312 | bytes 4718592 | tf_op jit(solution)/shard_map/pallas_call | solution.py:32
  374.3 20.4 %shard_map.174 = (bf16[2048,768]{1,0:T(8,128)(2,1)}, f32[768,3072]{1,0:T(8,128)}) custom-call(s32[4]{0:T(128)} %iota_xor_fusion.refs_0_, bf16[512,3072]{1,0:T(8,128)(2,1)} %get-tuple-element.28.refs_1_.refs_2_, bf16[256,3072]{1,0:T(8,128)(2,1)} %collective-permute-done.13.refs_3_.refs_2_, ...), custom_call_target="tpu_custom_call", output_to_operand_aliasing={{0}: (16, {})} | custom-call | flops 12079595520 | bytes 9437184 | tf_op jit(solution)/shard_map/pallas_call | solution.py:32
  (20 shorter events, 0.1 us)
Async XLA Ops:
  0.6 75.0 %collective-permute-start = (bf16[512,3072]{1,0:T(8,128)(2,1)}, bf16[512,3072]{1,0:T(8,128)(2,1)}, u32[]{:S(2)}, u32[]{:S(2)}) collective-permute-start(bf16[512,3072]{1,0:T(8,128)(2,1)} %refs_3_.8), channel_id=1, source_target_pairs={{0,1},{1,0},{2,3},{3,2},{4,5},{5,4},{6,7},{7,6}} | collective-permute-start | bytes 9437192 | tf_op jit(solution)/shard_map/ppermute | solution.py:354
  3.8 38.1 %collective-permute-start.4 = (bf16[256,3072]{1,0:T(8,128)(2,1)}, bf16[256,3072]{1,0:T(8,128)(2,1)}, u32[]{:S(2)}, u32[]{:S(2)}) collective-permute-start(bf16[256,3072]{1,0:T(8,128)(2,1)} %shard_map.163.refs_1_), channel_id=1, source_target_pairs={{0,2},{1,3},{2,0},{3,1},{4,6},{5,7},{6,4},{7,5}} | collective-permute-start | bytes 4718600 | tf_op jit(solution)/shard_map/ppermute | solution.py:357
  8.6 66.9 %collective-permute-start.2 = (bf16[256,3072]{1,0:T(8,128)(2,1)}, bf16[256,3072]{1,0:T(8,128)(2,1)}, u32[]{:S(2)}, u32[]{:S(2)}) collective-permute-start(bf16[256,3072]{1,0:T(8,128)(2,1)} %shard_map.164.refs_10_), channel_id=1, source_target_pairs={{0,2},{1,3},{2,0},{3,1},{4,6},{5,7},{6,4},{7,5}} | collective-permute-start | bytes 4718600 | tf_op jit(solution)/shard_map/ppermute | solution.py:357
  8.6 150.0 %collective-permute-start.10 = (bf16[512,3072]{1,0:T(8,128)(2,1)}, bf16[512,3072]{1,0:T(8,128)(2,1)}, u32[]{:S(2)}, u32[]{:S(2)}) collective-permute-start(bf16[512,3072]{1,0:T(8,128)(2,1)} %refs_0_.9), channel_id=1, source_target_pairs={{0,2},{1,3},{2,0},{3,1},{4,6},{5,7},{6,4},{7,5}} | collective-permute-start | bytes 9437192 | tf_op jit(solution)/shard_map/ppermute | solution.py:357
  41.9 85.6 %collective-permute-start.5 = (bf16[256,3072]{1,0:T(8,128)(2,1)}, bf16[256,3072]{1,0:T(8,128)(2,1)}, u32[]{:S(2)}, u32[]{:S(2)}) collective-permute-start(bf16[256,3072]{1,0:T(8,128)(2,1)} %collective-permute-done.4.refs_1_.refs_5_), channel_id=1, source_target_pairs={{0,1},{1,0},{2,3},{3,2},{4,5},{5,4},{6,7},{7,6}} | collective-permute-start | bytes 4718600 | tf_op jit(solution)/shard_map/ppermute | solution.py:354
  75.6 83.1 %collective-permute-start.3 = (bf16[256,3072]{1,0:T(8,128)(2,1)}, bf16[256,3072]{1,0:T(8,128)(2,1)}, u32[]{:S(2)}, u32[]{:S(2)}) collective-permute-start(bf16[256,3072]{1,0:T(8,128)(2,1)} %collective-permute-done.2.refs_1_.refs_7_), channel_id=1, source_target_pairs={{0,1},{1,0},{2,3},{3,2},{4,5},{5,4},{6,7},{7,6}} | collective-permute-start | bytes 4718600 | tf_op jit(solution)/shard_map/ppermute | solution.py:354
  157.6 3.9 collective-permute-start.6
  158.1 74.4 %collective-permute-start.9 = (bf16[512,3072]{1,0:T(8,128)(2,1)}, bf16[512,3072]{1,0:T(8,128)(2,1)}, u32[]{:S(2)}, u32[]{:S(2)}) collective-permute-start(bf16[512,3072]{1,0:T(8,128)(2,1)} %refs_0_.9), channel_id=1, source_target_pairs={{0,1},{1,0},{2,3},{3,2},{4,5},{5,4},{6,7},{7,6}} | collective-permute-start | bytes 9437192 | tf_op jit(solution)/shard_map/ppermute | solution.py:354
  158.1 74.4 %collective-permute-start.1 = (bf16[512,3072]{1,0:T(8,128)(2,1)}, bf16[512,3072]{1,0:T(8,128)(2,1)}, u32[]{:S(2)}, u32[]{:S(2)}) collective-permute-start(bf16[512,3072]{1,0:T(8,128)(2,1)} %get-tuple-element.35), channel_id=1, source_target_pairs={{0,1},{1,0},{2,3},{3,2},{4,5},{5,4},{6,7},{7,6}} | collective-permute-start | bytes 9437192 | tf_op jit(solution)/shard_map/ppermute | solution.py:354
  158.6 73.9 %collective-permute-start.11 = (bf16[512,3072]{1,0:T(8,128)(2,1)}, bf16[512,3072]{1,0:T(8,128)(2,1)}, u32[]{:S(2)}, u32[]{:S(2)}) collective-permute-start(bf16[512,3072]{1,0:T(8,128)(2,1)} %collective-permute-done.10.refs_2_), channel_id=1, source_target_pairs={{0,1},{1,0},{2,3},{3,2},{4,5},{5,4},{6,7},{7,6}} | collective-permute-start | bytes 9437192 | tf_op jit(solution)/shard_map/ppermute | solution.py:354
  193.2 35.7 %collective-permute-start.7 = (bf16[256,3072]{1,0:T(8,128)(2,1)}, bf16[256,3072]{1,0:T(8,128)(2,1)}, u32[]{:S(2)}, u32[]{:S(2)}) collective-permute-start(bf16[256,3072]{1,0:T(8,128)(2,1)} %get-tuple-element.39), channel_id=1, source_target_pairs={{0,1},{1,0},{2,3},{3,2},{4,5},{5,4},{6,7},{7,6}} | collective-permute-start | bytes 4718600 | tf_op jit(solution)/shard_map/ppermute | solution.py:354
  193.6 38.9 %collective-permute-start.12 = (bf16[256,3072]{1,0:T(8,128)(2,1)}, bf16[256,3072]{1,0:T(8,128)(2,1)}, u32[]{:S(2)}, u32[]{:S(2)}) collective-permute-start(bf16[256,3072]{1,0:T(8,128)(2,1)} %get-tuple-element.46), channel_id=1, source_target_pairs={{0,2},{1,3},{2,0},{3,1},{4,6},{5,7},{6,4},{7,5}} | collective-permute-start | bytes 4718600 | tf_op jit(solution)/shard_map/ppermute | solution.py:357
  232.5 52.9 %collective-permute-start.8 = (bf16[256,3072]{1,0:T(8,128)(2,1)}, bf16[256,3072]{1,0:T(8,128)(2,1)}, u32[]{:S(2)}, u32[]{:S(2)}) collective-permute-start(bf16[256,3072]{1,0:T(8,128)(2,1)} %add_convert_fusion.refs_17_), channel_id=1, source_target_pairs={{0,2},{1,3},{2,0},{3,1},{4,6},{5,7},{6,4},{7,5}} | collective-permute-start | bytes 4718600 | tf_op jit(solution)/shard_map/ppermute | solution.py:357
  259.6 44.2 %collective-permute-start.15 = (bf16[256,3072]{1,0:T(8,128)(2,1)}, bf16[256,3072]{1,0:T(8,128)(2,1)}, u32[]{:S(2)}, u32[]{:S(2)}) collective-permute-start(bf16[256,3072]{1,0:T(8,128)(2,1)} %get-tuple-element.53.refs_12_), channel_id=1, source_target_pairs={{0,2},{1,3},{2,0},{3,1},{4,6},{5,7},{6,4},{7,5}} | collective-permute-start | bytes 4718600 | tf_op jit(solution)/shard_map/ppermute | solution.py:357
  292.2 44.1 %collective-permute-start.17 = (bf16[256,3072]{1,0:T(8,128)(2,1)}, bf16[256,3072]{1,0:T(8,128)(2,1)}, u32[]{:S(2)}, u32[]{:S(2)}) collective-permute-start(bf16[256,3072]{1,0:T(8,128)(2,1)} %get-tuple-element.56.refs_12_), channel_id=1, source_target_pairs={{0,2},{1,3},{2,0},{3,1},{4,6},{5,7},{6,4},{7,5}} | collective-permute-start | bytes 4718600 | tf_op jit(solution)/shard_map/ppermute | solution.py:357
  292.3 67.6 %collective-permute-start.13 = (bf16[256,3072]{1,0:T(8,128)(2,1)}, bf16[256,3072]{1,0:T(8,128)(2,1)}, u32[]{:S(2)}, u32[]{:S(2)}) collective-permute-start(bf16[256,3072]{1,0:T(8,128)(2,1)} %get-tuple-element.53.refs_12_), channel_id=1, source_target_pairs={{0,1},{1,0},{2,3},{3,2},{4,5},{5,4},{6,7},{7,6}} | collective-permute-start | bytes 4718600 | tf_op jit(solution)/shard_map/ppermute | solution.py:354
  292.3 67.6 %collective-permute-start.14 = (bf16[256,3072]{1,0:T(8,128)(2,1)}, bf16[256,3072]{1,0:T(8,128)(2,1)}, u32[]{:S(2)}, u32[]{:S(2)}) collective-permute-start(bf16[256,3072]{1,0:T(8,128)(2,1)} %get-tuple-element.56.refs_12_), channel_id=1, source_target_pairs={{0,1},{1,0},{2,3},{3,2},{4,5},{5,4},{6,7},{7,6}} | collective-permute-start | bytes 4718600 | tf_op jit(solution)/shard_map/ppermute | solution.py:354
  303.8 56.1 %collective-permute-start.16 = (bf16[256,3072]{1,0:T(8,128)(2,1)}, bf16[256,3072]{1,0:T(8,128)(2,1)}, u32[]{:S(2)}, u32[]{:S(2)}) collective-permute-start(bf16[256,3072]{1,0:T(8,128)(2,1)} %collective-permute-done.15.refs_5_.refs_4_), channel_id=1, source_target_pairs={{0,1},{1,0},{2,3},{3,2},{4,5},{5,4},{6,7},{7,6}} | collective-permute-start | bytes 4718600 | tf_op jit(solution)/shard_map/ppermute | solution.py:354
  336.4 37.9 %collective-permute-start.18 = (bf16[256,3072]{1,0:T(8,128)(2,1)}, bf16[256,3072]{1,0:T(8,128)(2,1)}, u32[]{:S(2)}, u32[]{:S(2)}) collective-permute-start(bf16[256,3072]{1,0:T(8,128)(2,1)} %collective-permute-done.17.refs_6_), channel_id=1, source_target_pairs={{0,1},{1,0},{2,3},{3,2},{4,5},{5,4},{6,7},{7,6}} | collective-permute-start | bytes 4718600 | tf_op jit(solution)/shard_map/ppermute | solution.py:354

commit v3 on v2

--- a/solution.py
+++ b/solution.py
@@ -222,35 +222,48 @@
     return (grad_res[...].astype(F32) + inv_rms * (scaled - xin_f * (inv_rms * inv_rms) * proj_mean)).astype(BF16)
 
 
-def norm_chunk(parts, starts, rows, first_row, x_in, gamma, grad_res, prev, cuts, block=128, after=()):
+def norm_chunk(parts, starts, rows, first_row, x_in, gamma, grad_res, prev, block=64, after=()):
     width = x_in.shape[1]
-    n_cuts = len(cuts)
-    edges = [sum(cuts[:k]) // block for k in range(n_cuts + 1)]
-
-    def kernel(p0, p1, p2, xin, gam, res, *outs):
-        outs = outs[-1 - n_cuts:]
-        out = norm_rows(p0, p1, p2, xin, gam, res)
-        outs[-1][...] = out
-        for k in range(n_cuts):
-            @pl.when((pl.program_id(0) >= edges[k]) & (pl.program_id(0) < edges[k + 1]))
-            def _(k=k):
-                outs[k][...] = out
-
-    first = first_row // block
-    at = lambda s: pl.BlockSpec((block, width), lambda i: (s + i, 0))
-    cut = lambda k: pl.BlockSpec((block, width), lambda i: (jnp.clip(i - edges[k], 0, edges[k + 1] - edges[k] - 1), 0))
-    in_specs = [at(s // block) for s in starts] + [at(first), pl.BlockSpec((width,), lambda i: (0,)), at(first)]
-    args = [*parts, x_in, gamma, grad_res]
-    aliases = None
-    if prev is not None:
-        in_specs.append(pl.BlockSpec(memory_space=pl.ANY))
-        args.append(prev)
-        aliases = {len(in_specs) - 1: n_cuts}
-    return call(
-        kernel, (rows // block,), in_specs, [cut(k) for k in range(n_cuts)] + [at(first)],
-        [jax.ShapeDtypeStruct((c, width), BF16) for c in cuts] + [jax.ShapeDtypeStruct(x_in.shape, BF16)],
-        rows * width * 20, rows * width * 14, after=after, aliases=aliases,
-    )(*args)
+    n_blocks = rows // block
+    firsts = (*starts, first_row, first_row)
+
+    def kernel(p0, p1, p2, xin, res, gam, _, o_chunk, o_full, held, made, in_sem, out_sem):
+        srcs = (p0, p1, p2, xin, res)
+
+        def loads(b):
+            return [pltpu.make_async_copy(src.at[pl.ds(pl.multiple_of(first + b * block, block), block)], held.at[b, k], in_sem.at[b, k])
+                    for k, (src, first) in enumerate(zip(srcs, firsts))]
+
+        for b in range(n_blocks):
+            for copy in loads(b):
+                copy.start()
+
+        def store(b):
+            at = pl.multiple_of(b * block, block)
+            return [pltpu.make_async_copy(made.at[b], o_chunk.at[pl.ds(at, block)], out_sem.at[b, 0]),
+                    pltpu.make_async_copy(made.at[b], o_full.at[pl.ds(first_row + at, block)], out_sem.at[b, 1])]
+
+        def step(b, _):
+            for copy in loads(b):
+                copy.wait()
+            made[b] = norm_rows(held[b, 0], held[b, 1], held[b, 2], held[b, 3], gam, held[b, 4])
+            for copy in store(b):
+                copy.start()
+            return 0
+
+        lax.fori_loop(0, n_blocks, step, 0)
+        for b in range(n_blocks):
+            for copy in store(b):
+                copy.wait()
+
+    anywhere = pl.BlockSpec(memory_space=pl.ANY)
+    return call(
+        kernel, (1,), [anywhere] * 5 + [pl.BlockSpec((width,), lambda i: (0,)), anywhere], [anywhere] * 2,
+        [jax.ShapeDtypeStruct((rows, width), BF16), jax.ShapeDtypeStruct(x_in.shape, BF16)],
+        rows * width * 20, rows * width * 14, after=after, aliases={6: 1},
+        scratch=[pltpu.VMEM((n_blocks, 5, block, width), BF16), pltpu.VMEM((n_blocks, block, width), BF16),
+                 pltpu.SemaphoreType.DMA((n_blocks, 5)), pltpu.SemaphoreType.DMA((n_blocks, 2))],
+    )(*parts, x_in, grad_res, gamma, prev)
 
 
 def grad_attention(pieces, at_rows, blocks, w_out, offs, n_tok, group=2, after=()):
@@ -398,7 +411,7 @@
                              norm=(dx_own, dx_sib, rs[0], *norm), norm_size=half, after=(gwd, both[1]))
         s_acr0, s_par0 = send(ds0), swap(ds0)
         gw = gw_in(x_parts, gates, ups, (third, 2 * third), gw, 1024, 512, after=(ds0,))
-        ds1, ds = norm_chunk((dx_own, dx_sib, rs[1]), (half, half, 0), half, half, *norm, ds, (half,), after=(gw[0],))
+        ds1, ds = norm_chunk((dx_own, dx_sib, rs[1]), (half, half, 0), half, half, *norm, ds, after=(gw[0],))
         s_acr1, s_par1 = send(ds1), swap(ds1)
         gwg, gwu = gw_in(x_parts, gates, ups, (2 * third, width), gw, 1024, 512, after=(ds1,))
         s_dia0, s_dia1 = swap(s_acr0), swap(s_acr1)

time: 395 us -> 395 us (level)
  transfers between devices with their start and end apart: 19 -> 19, of which waited for: 5 -> 5; matrix products, arithmetic and copies ran while one was open for 1% -> 1% of each run, Pallas kernels for 63% -> 62%
where the time goes in v3:
time: 395 us
  Pallas kernels  267 us (68%)
  waiting for transfers between devices  112 us (28%)
  starting transfers between devices  11.5 us (3%)
  other arithmetic  4.08 us (1%)
    pallas_call x12, Pallas kernels, launch(): pl.pallas_call(body, grid_spec=pltpu.PrefetchScalarGridSpec(num_scalar_pr...  267 us
    ppermute x7, waiting for transfers between devices, send(): return lax.ppermute(x, 'tp', across)  109 us
    ppermute x7, starting transfers between devices, send(): return lax.ppermute(x, 'tp', across)  8.65 us
  transfers between devices with their start and end apart: 19, of which 5 were waited for; matrix products, arithmetic and copies ran while one was open for 1% of the time, Pallas kernels for 62%

profile of v3, /device:TPU:0, one launch (start us, length us, event | category | flops | bytes accessed | tf_op | source)
XLA Modules:
  0.0 394.9 jit_solution(4364521431981950904)
XLA Ops:
  0.6 0.9 collective-permute-start
  1.5 2.3 shard_map.163.refs_1_
  3.8 2.5 collective-permute-start.4
  6.3 2.3 shard_map.164.refs_10_
  8.6 2.0 collective-permute-start.10
  10.7 0.5 iota_xor_fusion.refs_0_
  11.1 30.7 %collective-permute-done.4.refs_1_.refs_5_ = bf16[256,3072]{1,0:T(8,128)(2,1)} collective-permute-done((bf16[256,3072]{1,0:T(8,128)(2,1)}, bf16[256,3072]{1,0:T(8,128)(2,1)}, u32[]{:S(2)}, u32[]{:S(2)}) %collective-permute-start.4) | collective-permute-done | bytes 1572896 | tf_op jit(solution)/shard_map/ppermute | solution.py:370
  41.9 33.7 %collective-permute-done.2.refs_1_.refs_7_ = bf16[256,3072]{1,0:T(8,128)(2,1)} collective-permute-done((bf16[256,3072]{1,0:T(8,128)(2,1)}, bf16[256,3072]{1,0:T(8,128)(2,1)}, u32[]{:S(2)}, u32[]{:S(2)}) %collective-permute-start.2) | collective-permute-done | bytes 1572896 | tf_op jit(solution)/shard_map/ppermute | solution.py:370
  75.6 51.9 %shard_map.165 = (bf16[1024,2048]{1,0:T(8,128)(2,1)}, bf16[1024,2048]{1,0:T(8,128)(2,1)}, bf16[1024,2048]{1,0:T(8,128)(2,1)}, bf16[512,3072]{1,0:T(8,128)(2,1)}, bf16[512,3072]{1,0:T(8,128)(2,1)}) custom-call(s32[4]{0:T(128)} %iota_xor_fusion.refs_0_, bf16[512,3072]{1,0:T(8,128)(2,1)} %refs_3_.8, bf16[512,3072]{1,0:T(8,128)(2,1)} %collective-permute-done.refs_2_.refs_4_, ...), custom_call_target="tpu_custom_call" | custom-call | flops 38654705664 | bytes 58720256 | tf_op jit(solution)/shard_map/pallas_call | solution.py:32
  127.5 30.0 %shard_map.166 = (bf16[512,2048]{1,0:T(8,128)(2,1)}, bf16[512,2048]{1,0:T(8,128)(2,1)}, bf16[512,2048]{1,0:T(8,128)(2,1)}, bf16[256,3072]{1,0:T(8,128)(2,1)}, bf16[256,3072]{1,0:T(8,128)(2,1)}) custom-call(s32[4]{0:T(128)} %iota_xor_fusion.refs_0_, bf16[256,3072]{1,0:T(8,128)(2,1)} %collective-permute-done.4.refs_1_.refs_5_, ...), custom_call_target="tpu_custom_call" | custom-call | flops 19327352832 | bytes 48234496 | tf_op jit(solution)/shard_map/pallas_call | solution.py:32
  157.6 0.5 collective-permute-start.6
  158.1 0.0 collective-permute-start.9
  158.1 0.5 collective-permute-start.1
  158.6 0.0 collective-permute-start.11
  158.7 2.8 collective-permute-done.6.refs_11_
  161.5 31.7 %shard_map.167 = (bf16[512,2048]{1,0:T(8,128)(2,1)}, bf16[512,2048]{1,0:T(8,128)(2,1)}, bf16[512,2048]{1,0:T(8,128)(2,1)}, bf16[256,3072]{1,0:T(8,128)(2,1)}, bf...) custom-call(s32[4]{0:T(128)} %iota_xor_fusion.refs_0_, bf16[256,3072]{1,0:T(8,128)(2,1)} %collective-permute-done.2.refs_1_.refs_7_, ...), custom_call_target="tpu_custom_call" | custom-call | flops 19327352832 | bytes 48234496 | tf_op jit(solution)/shard_map/pallas_call | solution.py:32
  193.2 0.4 collective-permute-start.7
  193.6 2.0 collective-permute-start.12
  195.6 33.2 %shard_map.168.refs_16_ = f32[2048,3072]{1,0:T(8,128)} custom-call(bf16[1024,2048]{1,0:T(8,128)(2,1)} %get-tuple-element.47.refs_0_, bf16[512,2048]{1,0:T(8,128)(2,1)} %get-tuple-element.48.refs_1_, bf16[512,2048]{1,0:T(8,128)(2,1)} %get-tuple-element.49.refs_2_, bf16[512,3072]{1,0:T(8,128)(2,1)} %refs_3_.8, ...), custom_call_target="tpu_custom_call" | custom-call | flops 25769803776 | bytes 25165824 | tf_op jit(solution)/shard_map/pallas_call | solution.py:32
  228.9 3.6 add_convert_fusion.refs_17_
  232.5 0.0 collective-permute-start.8
  232.5 27.1 %shard_map.169 = (bf16[256,3072]{1,0:T(8,128)(2,1)}, bf16[512,3072]{1,0:T(8,128)(2,1)}, f32[3072,2048]{1,0:T(8,128)}, f32[3072,2048]{1,0:T(8,128)}) custom-call(bf16[512,3072]{1,0:T(8,128)(2,1)} %refs_0_.9, bf16[512,3072]{1,0:T(8,128)(2,1)} %collective-permute-done.9.refs_1_, bf16[512,3072]{1,0:T(8,128)(2,1)} %collective-permute-done.10.refs_2_, ...), custom_call_target="tpu_custom_call" | custom-call | flops 17179869184 | bytes 16777216 | tf_op jit(solution)/shard_map/pallas_call | solution.py:32
  259.6 2.0 collective-permute-start.15
  261.6 23.7 %shard_map.170 = (f32[3072,2048]{1,0:T(8,128)}, f32[3072,2048]{1,0:T(8,128)}) custom-call(bf16[512,3072]{1,0:T(8,128)(2,1)} %refs_0_.9, bf16[512,3072]{1,0:T(8,128)(2,1)} %collective-permute-done.9.refs_1_, bf16[512,3072]{1,0:T(8,128)(2,1)} %collective-permute-done.10.refs_2_, ...), custom_call_target="tpu_custom_call", output_to_operand_aliasing={{0}: (10, {}), {1}: (11, {})} | custom-call | flops 17179869184 | bytes 16777216 | tf_op jit(solution)/shard_map/pallas_call | solution.py:32
  285.3 6.2 %shard_map.171 = (bf16[256,3072]{1,0:T(8,128)(2,1)}, bf16[512,3072]{1,0:T(8,128)(2,1)}) custom-call(bf16[512,3072]{1,0:T(8,128)(2,1)} %get-tuple-element.34.refs_10_.refs_0_, bf16[512,3072]{1,0:T(8,128)(2,1)} %collective-permute-done.1.refs_11_.refs_1_, bf16[256,3072]{1,0:T(8,128)(2,1)} %collective-permute-done.8.refs_2_, ...), custom_call_target="tpu_custom_call", output_to_operand_aliasing={{1}: (6, {})} | custom-call | flops 15728640 | bytes 11010048 | tf_op jit(solution)/shard_map/pallas_call | solution.py:32
  291.5 0.0 collective-permute-start.17
  291.6 0.5 collective-permute-start.14
  292.1 11.7 %collective-permute-done.15.refs_5_.refs_4_ = bf16[256,3072]{1,0:T(8,128)(2,1)} collective-permute-done((bf16[256,3072]{1,0:T(8,128)(2,1)}, bf16[256,3072]{1,0:T(8,128)(2,1)}, u32[]{:S(2)}, u32[]{:S(2)}) %collective-permute-start.15) | collective-permute-done | bytes 1572896 | tf_op jit(solution)/shard_map/ppermute | solution.py:370
  303.8 32.6 %collective-permute-done.17.refs_6_ = bf16[256,3072]{1,0:T(8,128)(2,1)} collective-permute-done((bf16[256,3072]{1,0:T(8,128)(2,1)}, bf16[256,3072]{1,0:T(8,128)(2,1)}, u32[]{:S(2)}, u32[]{:S(2)}) %collective-permute-start.17) | collective-permute-done | bytes 1572896 | tf_op jit(solution)/shard_map/ppermute | solution.py:370
  336.4 23.5 %shard_map.172 = (f32[3072,2048]{1,0:T(8,128)}, f32[3072,2048]{1,0:T(8,128)}) custom-call(bf16[512,3072]{1,0:T(8,128)(2,1)} %refs_0_.9, bf16[512,3072]{1,0:T(8,128)(2,1)} %collective-permute-done.9.refs_1_, bf16[512,3072]{1,0:T(8,128)(2,1)} %collective-permute-done.10.refs_2_, ...), custom_call_target="tpu_custom_call", output_to_operand_aliasing={{0}: (10, {}), {1}: (11, {})} | custom-call | flops 17179869184 | bytes 16777216 | tf_op jit(solution)/shard_map/pallas_call | solution.py:32
  359.9 14.4 %shard_map.173.refs_16_ = bf16[2048,768]{1,0:T(8,128)(2,1)} custom-call(s32[4]{0:T(128)} %iota_xor_fusion.refs_0_, bf16[512,3072]{1,0:T(8,128)(2,1)} %get-tuple-element.28.refs_1_.refs_2_, bf16[512,3072]{1,0:T(8,128)(2,1)} %get-tuple-element.28.refs_1_.refs_2_, bf16[256,3072]{1,0:T(8,128)(2,1)} %collective-permute-done.13.refs_3_.refs_2_, ...), custom_call_target="tpu_custom_call" | custom-call | flops 7247757312 | bytes 4718592 | tf_op jit(solution)/shard_map/pallas_call | solution.py:32
  374.3 20.4 %shard_map.174 = (bf16[2048,768]{1,0:T(8,128)(2,1)}, f32[768,3072]{1,0:T(8,128)}) custom-call(s32[4]{0:T(128)} %iota_xor_fusion.refs_0_, bf16[512,3072]{1,0:T(8,128)(2,1)} %get-tuple-element.28.refs_1_.refs_2_, bf16[256,3072]{1,0:T(8,128)(2,1)} %collective-permute-done.13.refs_3_.refs_2_, ...), custom_call_target="tpu_custom_call", output_to_operand_aliasing={{0}: (16, {})} | custom-call | flops 12079595520 | bytes 9437184 | tf_op jit(solution)/shard_map/pallas_call | solution.py:32
  (20 shorter events, 0.1 us)
Async XLA Ops:
  0.6 75.0 %collective-permute-start = (bf16[512,3072]{1,0:T(8,128)(2,1)}, bf16[512,3072]{1,0:T(8,128)(2,1)}, u32[]{:S(2)}, u32[]{:S(2)}) collective-permute-start(bf16[512,3072]{1,0:T(8,128)(2,1)} %refs_3_.8), channel_id=1, source_target_pairs={{0,1},{1,0},{2,3},{3,2},{4,5},{5,4},{6,7},{7,6}} | collective-permute-start | bytes 9437192 | tf_op jit(solution)/shard_map/ppermute | solution.py:367
  3.8 38.1 %collective-permute-start.4 = (bf16[256,3072]{1,0:T(8,128)(2,1)}, bf16[256,3072]{1,0:T(8,128)(2,1)}, u32[]{:S(2)}, u32[]{:S(2)}) collective-permute-start(bf16[256,3072]{1,0:T(8,128)(2,1)} %shard_map.163.refs_1_), channel_id=1, source_target_pairs={{0,2},{1,3},{2,0},{3,1},{4,6},{5,7},{6,4},{7,5}} | collective-permute-start | bytes 4718600 | tf_op jit(solution)/shard_map/ppermute | solution.py:370
  8.6 66.9 %collective-permute-start.2 = (bf16[256,3072]{1,0:T(8,128)(2,1)}, bf16[256,3072]{1,0:T(8,128)(2,1)}, u32[]{:S(2)}, u32[]{:S(2)}) collective-permute-start(bf16[256,3072]{1,0:T(8,128)(2,1)} %shard_map.164.refs_10_), channel_id=1, source_target_pairs={{0,2},{1,3},{2,0},{3,1},{4,6},{5,7},{6,4},{7,5}} | collective-permute-start | bytes 4718600 | tf_op jit(solution)/shard_map/ppermute | solution.py:370
  8.6 150.0 %collective-permute-start.10 = (bf16[512,3072]{1,0:T(8,128)(2,1)}, bf16[512,3072]{1,0:T(8,128)(2,1)}, u32[]{:S(2)}, u32[]{:S(2)}) collective-permute-start(bf16[512,3072]{1,0:T(8,128)(2,1)} %refs_0_.9), channel_id=1, source_target_pairs={{0,2},{1,3},{2,0},{3,1},{4,6},{5,7},{6,4},{7,5}} | collective-permute-start | bytes 9437192 | tf_op jit(solution)/shard_map/ppermute | solution.py:370
  41.9 85.6 %collective-permute-start.5 = (bf16[256,3072]{1,0:T(8,128)(2,1)}, bf16[256,3072]{1,0:T(8,128)(2,1)}, u32[]{:S(2)}, u32[]{:S(2)}) collective-permute-start(bf16[256,3072]{1,0:T(8,128)(2,1)} %collective-permute-done.4.refs_1_.refs_5_), channel_id=1, source_target_pairs={{0,1},{1,0},{2,3},{3,2},{4,5},{5,4},{6,7},{7,6}} | collective-permute-start | bytes 4718600 | tf_op jit(solution)/shard_map/ppermute | solution.py:367
  75.6 83.1 %collective-permute-start.3 = (bf16[256,3072]{1,0:T(8,128)(2,1)}, bf16[256,3072]{1,0:T(8,128)(2,1)}, u32[]{:S(2)}, u32[]{:S(2)}) collective-permute-start(bf16[256,3072]{1,0:T(8,128)(2,1)} %collective-permute-done.2.refs_1_.refs_7_), channel_id=1, source_target_pairs={{0,1},{1,0},{2,3},{3,2},{4,5},{5,4},{6,7},{7,6}} | collective-permute-start | bytes 4718600 | tf_op jit(solution)/shard_map/ppermute | solution.py:367
  157.6 3.9 collective-permute-start.6
  158.1 74.4 %collective-permute-start.9 = (bf16[512,3072]{1,0:T(8,128)(2,1)}, bf16[512,3072]{1,0:T(8,128)(2,1)}, u32[]{:S(2)}, u32[]{:S(2)}) collective-permute-start(bf16[512,3072]{1,0:T(8,128)(2,1)} %refs_0_.9), channel_id=1, source_target_pairs={{0,1},{1,0},{2,3},{3,2},{4,5},{5,4},{6,7},{7,6}} | collective-permute-start | bytes 9437192 | tf_op jit(solution)/shard_map/ppermute | solution.py:367
  158.1 74.4 %collective-permute-start.1 = (bf16[512,3072]{1,0:T(8,128)(2,1)}, bf16[512,3072]{1,0:T(8,128)(2,1)}, u32[]{:S(2)}, u32[]{:S(2)}) collective-permute-start(bf16[512,3072]{1,0:T(8,128)(2,1)} %get-tuple-element.35), channel_id=1, source_target_pairs={{0,1},{1,0},{2,3},{3,2},{4,5},{5,4},{6,7},{7,6}} | collective-permute-start | bytes 9437192 | tf_op jit(solution)/shard_map/ppermute | solution.py:367
  158.6 73.9 %collective-permute-start.11 = (bf16[512,3072]{1,0:T(8,128)(2,1)}, bf16[512,3072]{1,0:T(8,128)(2,1)}, u32[]{:S(2)}, u32[]{:S(2)}) collective-permute-start(bf16[512,3072]{1,0:T(8,128)(2,1)} %collective-permute-done.10.refs_2_), channel_id=1, source_target_pairs={{0,1},{1,0},{2,3},{3,2},{4,5},{5,4},{6,7},{7,6}} | collective-permute-start | bytes 9437192 | tf_op jit(solution)/shard_map/ppermute | solution.py:367
  193.2 35.7 %collective-permute-start.7 = (bf16[256,3072]{1,0:T(8,128)(2,1)}, bf16[256,3072]{1,0:T(8,128)(2,1)}, u32[]{:S(2)}, u32[]{:S(2)}) collective-permute-start(bf16[256,3072]{1,0:T(8,128)(2,1)} %get-tuple-element.39), channel_id=1, source_target_pairs={{0,1},{1,0},{2,3},{3,2},{4,5},{5,4},{6,7},{7,6}} | collective-permute-start | bytes 4718600 | tf_op jit(solution)/shard_map/ppermute | solution.py:367
  193.6 38.9 %collective-permute-start.12 = (bf16[256,3072]{1,0:T(8,128)(2,1)}, bf16[256,3072]{1,0:T(8,128)(2,1)}, u32[]{:S(2)}, u32[]{:S(2)}) collective-permute-start(bf16[256,3072]{1,0:T(8,128)(2,1)} %get-tuple-element.46), channel_id=1, source_target_pairs={{0,2},{1,3},{2,0},{3,1},{4,6},{5,7},{6,4},{7,5}} | collective-permute-start | bytes 4718600 | tf_op jit(solution)/shard_map/ppermute | solution.py:370
  232.5 52.9 %collective-permute-start.8 = (bf16[256,3072]{1,0:T(8,128)(2,1)}, bf16[256,3072]{1,0:T(8,128)(2,1)}, u32[]{:S(2)}, u32[]{:S(2)}) collective-permute-start(bf16[256,3072]{1,0:T(8,128)(2,1)} %add_convert_fusion.refs_17_), channel_id=1, source_target_pairs={{0,2},{1,3},{2,0},{3,1},{4,6},{5,7},{6,4},{7,5}} | collective-permute-start | bytes 4718600 | tf_op jit(solution)/shard_map/ppermute | solution.py:370
  259.6 44.2 %collective-permute-start.15 = (bf16[256,3072]{1,0:T(8,128)(2,1)}, bf16[256,3072]{1,0:T(8,128)(2,1)}, u32[]{:S(2)}, u32[]{:S(2)}) collective-permute-start(bf16[256,3072]{1,0:T(8,128)(2,1)} %get-tuple-element.53.refs_12_), channel_id=1, source_target_pairs={{0,2},{1,3},{2,0},{3,1},{4,6},{5,7},{6,4},{7,5}} | collective-permute-start | bytes 4718600 | tf_op jit(solution)/shard_map/ppermute | solution.py:370
  291.5 44.8 %collective-permute-start.17 = (bf16[256,3072]{1,0:T(8,128)(2,1)}, bf16[256,3072]{1,0:T(8,128)(2,1)}, u32[]{:S(2)}, u32[]{:S(2)}) collective-permute-start(bf16[256,3072]{1,0:T(8,128)(2,1)} %get-tuple-element.56.refs_12_), channel_id=1, source_target_pairs={{0,2},{1,3},{2,0},{3,1},{4,6},{5,7},{6,4},{7,5}} | collective-permute-start | bytes 4718600 | tf_op jit(solution)/shard_map/ppermute | solution.py:370
  291.6 68.3 %collective-permute-start.13 = (bf16[256,3072]{1,0:T(8,128)(2,1)}, bf16[256,3072]{1,0:T(8,128)(2,1)}, u32[]{:S(2)}, u32[]{:S(2)}) collective-permute-start(bf16[256,3072]{1,0:T(8,128)(2,1)} %get-tuple-element.53.refs_12_), channel_id=1, source_target_pairs={{0,1},{1,0},{2,3},{3,2},{4,5},{5,4},{6,7},{7,6}} | collective-permute-start | bytes 4718600 | tf_op jit(solution)/shard_map/ppermute | solution.py:367
  291.6 68.3 %collective-permute-start.14 = (bf16[256,3072]{1,0:T(8,128)(2,1)}, bf16[256,3072]{1,0:T(8,128)(2,1)}, u32[]{:S(2)}, u32[]{:S(2)}) collective-permute-start(bf16[256,3072]{1,0:T(8,128)(2,1)} %get-tuple-element.56.refs_12_), channel_id=1, source_target_pairs={{0,1},{1,0},{2,3},{3,2},{4,5},{5,4},{6,7},{7,6}} | collective-permute-start | bytes 4718600 | tf_op jit(solution)/shard_map/ppermute | solution.py:367
  303.8 56.1 %collective-permute-start.16 = (bf16[256,3072]{1,0:T(8,128)(2,1)}, bf16[256,3072]{1,0:T(8,128)(2,1)}, u32[]{:S(2)}, u32[]{:S(2)}) collective-permute-start(bf16[256,3072]{1,0:T(8,128)(2,1)} %collective-permute-done.15.refs_5_.refs_4_), channel_id=1, source_target_pairs={{0,1},{1,0},{2,3},{3,2},{4,5},{5,4},{6,7},{7,6}} | collective-permute-start | bytes 4718600 | tf_op jit(solution)/shard_map/ppermute | solution.py:367
  336.4 37.9 %collective-permute-start.18 = (bf16[256,3072]{1,0:T(8,128)(2,1)}, bf16[256,3072]{1,0:T(8,128)(2,1)}, u32[]{:S(2)}, u32[]{:S(2)}) collective-permute-start(bf16[256,3072]{1,0:T(8,128)(2,1)} %collective-permute-done.17.refs_6_), channel_id=1, source_target_pairs={{0,1},{1,0},{2,3},{3,2},{4,5},{5,4},{6,7},{7,6}} | collective-permute-start | bytes 4718600 | tf_op jit(solution)/shard_map/ppermute | solution.py:367
